TPU v7x, 128 devices: a whole 4x4x4 slice. The times are simulated.
128 devices in a mesh: grp: 2 (over core), dev: 64 (over x, z, y).
Axes of the slice: x: 4, y: 4, z: 4, core: 2. Of those that a mesh axis runs over, the one named last changes fastest.
Arguments:
- state: float32 [2, 24, 24, 16384], P(None, None, None, ('grp', 'dev')), may hold values from -6 to 6
- hamiltonian: float32 [24, 24], replicated, may hold values from -1.2 to 1.2
- mode_rates: float32 [96], replicated, may hold values from 0.05 to 2
- ado_modes: int32 [3, 16384], P(None, ('grp', 'dev')), may hold values from 0 to 96
- link_src: int32 [8, 16384], P(None, ('grp', 'dev')), may hold values from 0 to 383, as said below
- link_site: int32 [8, 16384], P(None, ('grp', 'dev')), may hold values from 0 to 23
- link_coef: float32 [4, 8, 16384], P(None, None, ('grp', 'dev')), may hold values from -2.4 to 2.4
- send_ids: int32 [128, 256], P(('grp', 'dev')), may hold values from 0 to 127
- step_units: int32 [], replicated, may hold values from 12 to 16
Outputs:
- new_state: float32 [2, 24, 24, 16384], P(None, None, None, ('grp', 'dev'))
- error_norm: float32 [], replicated
Inputs may be any that keep to these rules, and one draw needn't show every extreme that they name: `link_src`: on each device every received position 128 to 383 is named by 1 to 4 couplings of that device's matrices, and some position by exactly 4.
All inputs are finite; a program needn't handle non-finite values.
Results may differ from a plain program's by a relative error of at most 0.0003.
Values sent between devices are 32-bit elements; how exact they have to be, the bound alone decides.
No kernel may reach another device: no remote copies, remote signals or barrier semaphores. Data moves between devices by JAX's collectives and lax.ppermute only.
A program may use at most 128 MiB of HBM per device.

v0:
```python
import functools

import jax
import jax.numpy as jnp
from jax import lax
from jax.sharding import Mesh
from jax.sharding import PartitionSpec as P

DEV = ("dev_0", "dev_1", "dev_2")
GRP_DEV = ("grp", "dev_0", "dev_1", "dev_2")


TABLEAU = (
    (0.2,),
    (3.0 / 40, 9.0 / 40),
    (44.0 / 45, -56.0 / 15, 32.0 / 9),
    (19372.0 / 6561, -25360.0 / 2187, 64448.0 / 6561, -212.0 / 729),
    (9017.0 / 3168, -355.0 / 33, 46732.0 / 5247, 49.0 / 176, -5103.0 / 18656),
    (35.0 / 384, 0.0, 500.0 / 1113, 125.0 / 192, -2187.0 / 6784, 11.0 / 84),
)
ERRORS = (71.0 / 57600, 0.0, -71.0 / 16695, 71.0 / 1920, -17253.0 / 339200, 22.0 / 525, -1.0 / 40)
ABS_TOL = 0.001
REL_TOL = 0.01
UNIT_STEP = 1.0 / 64
HIGHEST = lax.Precision.HIGHEST


def one_axis_at_a_time(shard, axes):
    return functools.reduce(lax.psum, axes, shard)


def commute(symmetric, current):
    left_prod = jnp.einsum("ab,sbcx->sacx", symmetric, current, precision=HIGHEST)
    right_prod = jnp.einsum("sabx,bc->sacx", current, symmetric, precision=HIGHEST)
    return left_prod - right_prod


def decay_rates(ado_modes, mode_rates):
    extended = jnp.concatenate([mode_rates, jnp.zeros((1,), mode_rates.dtype)])
    levels = jnp.arange(extended.shape[0], dtype=jnp.int32)
    hits = (ado_modes[:, None, :] == levels[None, :, None]).astype(mode_rates.dtype)
    return jnp.sum(hits * extended[None, :, None], axis=(0, 1))


def selector(indices, count, dtype):
    levels = jnp.arange(count, dtype=jnp.int32)
    return (levels[:, None] == indices.reshape(-1)[None, :]).astype(dtype)


def masked_term(source, sites, coef):
    levels = jnp.arange(source.shape[1], dtype=jnp.int32)
    indicator = (levels[:, None] == sites[None, :]).astype(source.dtype)
    row_mask = indicator[:, None, :]
    column_mask = indicator[None, :, :]
    weight_real = coef[0] * row_mask - coef[2] * column_mask
    weight_imag = coef[1] * row_mask - coef[3] * column_mask
    real_part = weight_real * source[0] - weight_imag * source[1]
    imag_part = weight_real * source[1] + weight_imag * source[0]
    return jnp.stack([imag_part, -real_part])


def shards(
    state, hamiltonian, mode_rates, ado_modes, link_src, link_site, link_coef, send_ids, step_units
):
    outgoing = send_ids[0]
    symmetric = 0.5 * (hamiltonian + hamiltonian.T)
    decay = decay_rates(ado_modes, mode_rates)
    step_size = step_units.astype(state.dtype) * UNIT_STEP
    groups = lax.axis_size("grp")
    members = lax.axis_size(DEV)
    sites = state.shape[1]
    owned = state.shape[3]
    received = outgoing.shape[0]
    links = link_src.shape[0]
    flat_rows = 2 * sites * sites
    pack_table = selector(outgoing, owned, state.dtype)
    link_table = selector(link_src, owned + received, state.dtype)

    def evaluate(current):
        flat_current = current.reshape(flat_rows, owned)
        packed = jnp.dot(flat_current, pack_table, precision=HIGHEST).reshape(
            2, sites, sites, received
        )
        commutator = commute(symmetric, current)
        total = jnp.stack([commutator[1], -commutator[0]]) - decay[None, None, None, :] * current
        moved = lax.all_to_all(packed, GRP_DEV, split_axis=3, concat_axis=3, tiled=True)
        combined = jnp.concatenate([flat_current, moved.reshape(flat_rows, received)], axis=1)
        fetched = jnp.dot(combined, link_table, precision=HIGHEST)
        for link in range(links):
            start = link * owned
            source = fetched[:, start : start + owned].reshape(2, sites, sites, owned)
            total = total + masked_term(source, link_site[link], link_coef[:, link])
        return total

    sections = [evaluate(state)]
    inner = state
    for weights in TABLEAU:
        inner = state
        for weight, section in zip(weights, sections):
            if weight != 0.0:
                inner = inner + step_size * weight * section
        sections.append(evaluate(inner))
    error = jnp.zeros_like(state)
    for weight, section in zip(ERRORS, sections):
        if weight != 0.0:
            error = error + step_size * weight * section
    scale = ABS_TOL + REL_TOL * jnp.maximum(jnp.abs(state), jnp.abs(inner))
    partial_sum = jnp.sum(jnp.square(error / scale))
    total_sum = one_axis_at_a_time(partial_sum, GRP_DEV)
    entries = 2 * sites * sites * owned * groups * members
    return (inner, jnp.sqrt(total_sum / entries))


def solution(mesh):
    finer = Mesh(
        mesh.devices.reshape(mesh.shape["grp"], 4, 4, 4), ("grp", "dev_0", "dev_1", "dev_2")
    )
    return jax.shard_map(
        shards,
        mesh=finer,
        in_specs=(
            P(None, None, None, GRP_DEV),
            P(),
            P(),
            P(None, GRP_DEV),
            P(None, GRP_DEV),
            P(None, GRP_DEV),
            P(None, None, GRP_DEV),
            P(GRP_DEV, None),
            P(),
        ),
        out_specs=(P(None, None, None, GRP_DEV), P()),
        check_vma=False,
    )
```

profile of v0, /device:TPU:0, one launch (start us, length us, event | category | flops | bytes accessed | tf_op | source)
XLA Modules:
  0.0 502.8 jit_solution(1082587879265455247)
XLA Ops:
  8.1 7.2 %reshape.4447 = f32[128,1,2304]{2,1,0:T(1,128)} reshape(f32[256,2,24,24]{3,2,1,0:T(8,128)} %bitcast.336) | data formatting | bytes 2359296
  15.4 11.7 %all-to-all-start = ((f32[128,1,2304]{2,1,0:T(1,128)}), f32[128,1,2304]{2,1,0:T(1,128)S(1)}, u32[]{:S(2)}, u32[]{:S(2)}) async-start(f32[128,1,2304]{2,1,0:T(1,128)} %reshape.4447), calls=%async_computation | async-start | bytes 2359296 | tf_op jit(solution)/shard_map/all_to_all | solution.py:86
  33.5 13.0 %all-to-all-done = f32[128,1,2304]{2,1,0:T(1,128)S(1)} async-done(((f32[128,1,2304]{2,1,0:T(1,128)}), f32[128,1,2304]{2,1,0:T(1,128)S(1)}, u32[]{:S(2)}, u32[]{:S(2)}) %all-to-all-start) | async-done | bytes 1179680 | tf_op jit(solution)/shard_map/all_to_all | solution.py:86
  50.4 6.3 %reshape.4448 = f32[256,2,24,24]{3,2,1,0:T(8,128)} reshape(f32[128,2304]{1,0:T(8,128)S(1)} %reduce) | data formatting | bytes 2359296
  75.8 7.2 %reshape.4449 = f32[128,1,2304]{2,1,0:T(1,128)} reshape(f32[256,2,24,24]{3,2,1,0:T(8,128)} %bitcast.338) | data formatting | bytes 2359296
  91.5 16.6 %all-to-all-done.1 = f32[128,1,2304]{2,1,0:T(1,128)} async-done(((f32[128,1,2304]{2,1,0:T(1,128)}), f32[128,1,2304]{2,1,0:T(1,128)}, u32[]{:S(2)}, u32[]{:S(2)}) %all-to-all-start.1) | async-done | bytes 1179680 | tf_op jit(solution)/shard_map/all_to_all | solution.py:86
  112.9 6.3 %reshape.4450 = f32[256,2,24,24]{3,2,1,0:T(8,128)} reshape(f32[128,2304]{1,0:T(8,128)S(1)} %reduce.1) | data formatting | bytes 2359296
  138.9 7.2 %reshape.4451 = f32[128,1,2304]{2,1,0:T(1,128)} reshape(f32[256,2,24,24]{3,2,1,0:T(8,128)} %bitcast.340) | data formatting | bytes 2359296
  146.1 6.4 %all-to-all-start.2 = ((f32[128,1,2304]{2,1,0:T(1,128)}), f32[128,1,2304]{2,1,0:T(1,128)}, u32[]{:S(2)}, u32[]{:S(2)}) async-start(f32[128,1,2304]{2,1,0:T(1,128)} %reshape.4451), calls=%async_computation.2 | async-start | bytes 2359296 | tf_op jit(solution)/shard_map/all_to_all | solution.py:86
  154.9 16.6 %all-to-all-done.2 = f32[128,1,2304]{2,1,0:T(1,128)} async-done(((f32[128,1,2304]{2,1,0:T(1,128)}), f32[128,1,2304]{2,1,0:T(1,128)}, u32[]{:S(2)}, u32[]{:S(2)}) %all-to-all-start.2) | async-done | bytes 1179680 | tf_op jit(solution)/shard_map/all_to_all | solution.py:86
  176.2 6.3 %reshape.4452 = f32[256,2,24,24]{3,2,1,0:T(8,128)} reshape(f32[128,2304]{1,0:T(8,128)S(1)} %reduce.2) | data formatting | bytes 2359296
  201.8 7.2 %reshape.4453 = f32[128,1,2304]{2,1,0:T(1,128)} reshape(f32[256,2,24,24]{3,2,1,0:T(8,128)} %bitcast.342) | data formatting | bytes 2359296
  218.4 15.8 %all-to-all-done.3 = f32[128,1,2304]{2,1,0:T(1,128)} async-done(((f32[128,1,2304]{2,1,0:T(1,128)}), f32[128,1,2304]{2,1,0:T(1,128)}, u32[]{:S(2)}, u32[]{:S(2)}) %all-to-all-start.3) | async-done | bytes 1179680 | tf_op jit(solution)/shard_map/all_to_all | solution.py:86
  238.9 6.3 %reshape.4454 = f32[256,2,24,24]{3,2,1,0:T(8,128)} reshape(f32[128,2304]{1,0:T(8,128)S(1)} %reduce.3) | data formatting | bytes 2359296
  261.8 6.3 %copy.1048 = f32[2,24,24,256]{2,1,0,3:T(8,128)} copy(f32[2,24,24,256]{3,1,2,0:T(8,128)} %fusion.278) | data formatting | bytes 2359296 | tf_op jit(solution)/shard_map/dot_general | solution.py:81
  268.1 7.2 %reshape.4455 = f32[128,1,2304]{2,1,0:T(1,128)} reshape(f32[256,2,24,24]{3,2,1,0:T(8,128)} %bitcast.344) | data formatting | bytes 2359296
  275.4 6.4 %all-to-all-start.4 = ((f32[128,1,2304]{2,1,0:T(1,128)}), f32[128,1,2304]{2,1,0:T(1,128)}, u32[]{:S(2)}, u32[]{:S(2)}) async-start(f32[128,1,2304]{2,1,0:T(1,128)} %reshape.4455), calls=%async_computation.4 | async-start | bytes 2359296 | tf_op jit(solution)/shard_map/all_to_all | solution.py:86
  284.1 16.6 %all-to-all-done.4 = f32[128,1,2304]{2,1,0:T(1,128)} async-done(((f32[128,1,2304]{2,1,0:T(1,128)}), f32[128,1,2304]{2,1,0:T(1,128)}, u32[]{:S(2)}, u32[]{:S(2)}) %all-to-all-start.4) | async-done | bytes 1179680 | tf_op jit(solution)/shard_map/all_to_all | solution.py:86
  306.5 6.7 %reshape.4456 = f32[256,2,24,24]{3,2,1,0:T(8,128)} reshape(f32[128,2304]{1,0:T(8,128)} %reduce.4) | data formatting | bytes 2359296
  331.3 6.3 %copy.1088 = f32[2,24,24,256]{2,1,0,3:T(8,128)} copy(f32[2,24,24,256]{3,1,2,0:T(8,128)} %fusion.276) | data formatting | bytes 2359296 | tf_op jit(solution)/shard_map/dot_general | solution.py:81
  337.6 7.2 %reshape.4457 = f32[128,1,2304]{2,1,0:T(1,128)} reshape(f32[256,2,24,24]{3,2,1,0:T(8,128)} %bitcast.346) | data formatting | bytes 2359296
  354.1 15.8 %all-to-all-done.5 = f32[128,1,2304]{2,1,0:T(1,128)} async-done(((f32[128,1,2304]{2,1,0:T(1,128)}), f32[128,1,2304]{2,1,0:T(1,128)}, u32[]{:S(2)}, u32[]{:S(2)}) %all-to-all-start.5) | async-done | bytes 1179680 | tf_op jit(solution)/shard_map/all_to_all | solution.py:86
  375.7 6.7 %reshape.4458 = f32[256,2,24,24]{3,2,1,0:T(8,128)} reshape(f32[128,2304]{1,0:T(8,128)} %reduce.5) | data formatting | bytes 2359296
  382.5 6.3 %copy.1089 = f32[2,24,24,256]{3,2,1,0:T(8,128)} copy(f32[2,24,24,256]{2,1,0,3:T(8,128)} %bitcast.347) | data formatting | bytes 2359296 | tf_op jit(solution)/shard_map/all_to_all | solution.py:86
  400.4 6.3 %copy.1127 = f32[2,24,24,256]{2,1,0,3:T(8,128)} copy(f32[2,24,24,256]{3,1,2,0:T(8,128)} %fusion.274) | data formatting | bytes 2359296 | tf_op jit(solution)/shard_map/dot_general | solution.py:81
  406.8 7.2 %reshape.4459 = f32[128,1,2304]{2,1,0:T(1,128)} reshape(f32[256,2,24,24]{3,2,1,0:T(8,128)} %bitcast.348) | data formatting | bytes 2359296
  414.0 6.4 %all-to-all-start.6 = ((f32[128,1,2304]{2,1,0:T(1,128)}), f32[128,1,2304]{2,1,0:T(1,128)}, u32[]{:S(2)}, u32[]{:S(2)}) async-start(f32[128,1,2304]{2,1,0:T(1,128)} %reshape.4459), calls=%async_computation.6 | async-start | bytes 2359296 | tf_op jit(solution)/shard_map/all_to_all | solution.py:86
  422.8 16.6 %all-to-all-done.6 = f32[128,1,2304]{2,1,0:T(1,128)} async-done(((f32[128,1,2304]{2,1,0:T(1,128)}), f32[128,1,2304]{2,1,0:T(1,128)}, u32[]{:S(2)}, u32[]{:S(2)}) %all-to-all-start.6) | async-done | bytes 1179680 | tf_op jit(solution)/shard_map/all_to_all | solution.py:86
  445.2 6.7 %reshape.4460 = f32[256,2,24,24]{3,2,1,0:T(8,128)} reshape(f32[128,2304]{1,0:T(8,128)} %reduce.6) | data formatting | bytes 2359296
  471.3 9.9 %psum.29 = f32[]{:T(128)} all-reduce(f32[]{:T(128)} %psum.28), channel_id=1, replica_groups=mesh['grp'=2,'dev_0'=4,'dev_1'=4,'dev_2'=4] {'dev_0'}, use_global_device_ids=true, to_apply=%region_3.0 | all-reduce | flops 1 | bytes 8 | tf_op jit(solution)/shard_map/psum | solution.py:29
  481.2 9.7 %psum.30 = f32[]{:T(128)} all-reduce(f32[]{:T(128)} %psum.29), channel_id=1, replica_groups=mesh['grp'=2,'dev_0'=4,'dev_1'=4,'dev_2'=4] {'dev_1'}, use_global_device_ids=true, to_apply=%region_4.0 | all-reduce | flops 1 | bytes 8 | tf_op jit(solution)/shard_map/psum | solution.py:29
  490.9 10.0 %psum.31 = f32[]{:T(128)} all-reduce(f32[]{:T(128)} %psum.30), channel_id=1, replica_groups=mesh['grp'=2,'dev_0'=4,'dev_1'=4,'dev_2'=4] {'dev_2'}, use_global_device_ids=true, to_apply=%region_5.0 | all-reduce | flops 1 | bytes 8 | tf_op jit(solution)/shard_map/psum | solution.py:29
  (679 shorter events, 203.7 us)
Async XLA Ops:
  15.4 11.7 %copy-start.263 = (f32[4,8,128]{2,1,0:T(8,128)S(1)}, f32[4,8,128]{2,1,0:T(8,128)}, u32[]{:S(2)}) copy-start(f32[4,8,128]{2,1,0:T(8,128)} %param.15) | copy-start | bytes 49156
  15.4 12.4 %copy-start.264 = (s32[8,128]{1,0:T(8,128)S(1)}, s32[8,128]{1,0:T(8,128)}, u32[]{:S(2)}) copy-start(s32[8,128]{1,0:T(8,128)} %param.14) | copy-start | bytes 12292
  15.4 12.5 %copy-start.255 = (f32[24,24]{1,0:T(8,128)S(1)}, f32[24,24]{1,0:T(8,128)}, u32[]{:S(2)}) copy-start(f32[24,24]{1,0:T(8,128)} %param.10) | copy-start | bytes 6916
  15.4 12.5 %copy-start.266 = (f32[96]{0:T(128)S(1)}, f32[96]{0:T(128)}, u32[]{:S(2)}) copy-start(f32[96]{0:T(128)} %param.11) | copy-start | bytes 1156
  15.4 12.6 %copy-start.265 = (s32[3,128]{1,0:T(4,128)S(1)}, s32[3,128]{1,0:T(4,128)}, u32[]{:S(2)}) copy-start(s32[3,128]{1,0:T(4,128)} %param.12) | copy-start | bytes 4612
  15.4 15.9 %copy-start = (f32[2,24,24,128]{3,2,1,0:T(8,128)S(1)}, f32[2,24,24,128]{3,2,1,0:T(8,128)}, u32[]{:S(2)}) copy-start(f32[2,24,24,128]{3,2,1,0:T(8,128)} %param.9) | copy-start | bytes 1769476
  15.4 31.1 %all-to-all-start = ((f32[128,1,2304]{2,1,0:T(1,128)}), f32[128,1,2304]{2,1,0:T(1,128)S(1)}, u32[]{:S(2)}, u32[]{:S(2)}) async-start(f32[128,1,2304]{2,1,0:T(1,128)} %reshape.4447), calls=%async_computation | async-start | bytes 2359296 | tf_op jit(solution)/shard_map/all_to_all | solution.py:86
  56.7 5.2 %copy-start.248 = (s32[8,128]{1,0:T(8,128)S(1)}, s32[8,128]{1,0:T(8,128)}, u32[]{:S(2)}) copy-start(s32[8,128]{1,0:T(8,128)} %param.13) | copy-start | bytes 12292
  83.0 25.2 %all-to-all-start.1 = ((f32[128,1,2304]{2,1,0:T(1,128)}), f32[128,1,2304]{2,1,0:T(1,128)}, u32[]{:S(2)}, u32[]{:S(2)}) async-start(f32[128,1,2304]{2,1,0:T(1,128)} %reshape.4449), calls=%async_computation.1 | async-start | bytes 2359296 | tf_op jit(solution)/shard_map/all_to_all | solution.py:86
  146.1 25.4 %all-to-all-start.2 = ((f32[128,1,2304]{2,1,0:T(1,128)}), f32[128,1,2304]{2,1,0:T(1,128)}, u32[]{:S(2)}, u32[]{:S(2)}) async-start(f32[128,1,2304]{2,1,0:T(1,128)} %reshape.4451), calls=%async_computation.2 | async-start | bytes 2359296 | tf_op jit(solution)/shard_map/all_to_all | solution.py:86
  193.8 1.2 copy-start.17
  193.8 1.2 copy-start.258
  209.0 25.2 %all-to-all-start.3 = ((f32[128,1,2304]{2,1,0:T(1,128)}), f32[128,1,2304]{2,1,0:T(1,128)}, u32[]{:S(2)}, u32[]{:S(2)}) async-start(f32[128,1,2304]{2,1,0:T(1,128)} %reshape.4453), calls=%async_computation.3 | async-start | bytes 2359296 | tf_op jit(solution)/shard_map/all_to_all | solution.py:86
  257.6 1.2 copy-start.259
  258.8 1.3 copy-start.252
  275.4 25.4 %all-to-all-start.4 = ((f32[128,1,2304]{2,1,0:T(1,128)}), f32[128,1,2304]{2,1,0:T(1,128)}, u32[]{:S(2)}, u32[]{:S(2)}) async-start(f32[128,1,2304]{2,1,0:T(1,128)} %reshape.4455), calls=%async_computation.4 | async-start | bytes 2359296 | tf_op jit(solution)/shard_map/all_to_all | solution.py:86
  326.6 1.2 copy-start.4
  326.6 1.3 copy-start.12
  326.6 1.4 copy-start.13
  326.6 1.4 copy-start.260
  328.0 1.5 copy-start.253
  344.8 25.2 %all-to-all-start.5 = ((f32[128,1,2304]{2,1,0:T(1,128)}), f32[128,1,2304]{2,1,0:T(1,128)}, u32[]{:S(2)}, u32[]{:S(2)}) async-start(f32[128,1,2304]{2,1,0:T(1,128)} %reshape.4457), calls=%async_computation.5 | async-start | bytes 2359296 | tf_op jit(solution)/shard_map/all_to_all | solution.py:86
  382.5 6.3 %copy-start.9 = (f32[2,24,24,128]{3,2,1,0:T(8,128)S(1)}, f32[2,24,24,128]{3,2,1,0:T(8,128)}, u32[]{:S(2)}) copy-start(f32[2,24,24,128]{3,2,1,0:T(8,128)} %copy.1084) | copy-start | bytes 1769476
  396.0 1.2 copy-start.15
  396.0 1.2 copy-start.261
  397.2 1.5 copy-start.254
  414.0 25.4 %all-to-all-start.6 = ((f32[128,1,2304]{2,1,0:T(1,128)}), f32[128,1,2304]{2,1,0:T(1,128)}, u32[]{:S(2)}, u32[]{:S(2)}) async-start(f32[128,1,2304]{2,1,0:T(1,128)} %reshape.4459), calls=%async_computation.6 | async-start | bytes 2359296 | tf_op jit(solution)/shard_map/all_to_all | solution.py:86
  420.5 37.5 %copy-start.7 = (f32[2,24,24,128]{3,2,1,0:T(8,128)}, f32[2,24,24,128]{3,2,1,0:T(8,128)S(1)}, u32[]{:S(2)}) copy-start(f32[2,24,24,128]{3,2,1,0:T(8,128)S(1)} %copy.1162) | copy-start | bytes 1769476
  465.3 1.2 copy-start.8
  465.3 1.3 copy-start.10
  465.3 1.4 copy-start.11
  465.3 1.4 copy-start.262
  (242 other events, 186.8 us)
where the time goes:
time: 509 us; the launch traced here: 503 us
  local copies, waits for them, and re-layouts  194 us (38%)
  waiting for transfers between devices  111 us (22%)
  other arithmetic  59.6 us (12%)
  matrix products  50.3 us (10%)
  starting transfers between devices  49.4 us (10%)
  blocking collectives  32.6 us (6%)
  between operations  6.2 us (1%)
    all_to_all x7, waiting for transfers between devices, evaluate(): lax.all_to_all(packed, GRP_DEV, split_axis=3, concat_axis=3, tiled=True)  111 us
    unnamed x550, local copies, waits for them, and re-layouts  107 us
    all_to_all x7, starting transfers between devices, evaluate(): lax.all_to_all(packed, GRP_DEV, split_axis=3, concat_axis=3, tiled=True)  49.4 us
    all_to_all x8, local copies, waits for them, and re-layouts, evaluate(): lax.all_to_all(packed, GRP_DEV, split_axis=3, concat_axis=3, tiled=True)  40.2 us
    dot_general x7, local copies, waits for them, and re-layouts, evaluate(): jnp.dot(flat_current, pack_table, precision=HIGHEST)  35.6 us
    all_to_all x7, other arithmetic, evaluate(): lax.all_to_all(packed, GRP_DEV, split_axis=3, concat_axis=3, tiled=True)  34.9 us
    psum x4, blocking collectives, one_axis_at_a_time(): return functools.reduce(lax.psum, axes, shard)  32.6 us
    dot_general x7, matrix products, evaluate(): fetched = jnp.dot(combined, link_table, precision=HIGHEST)  32.2 us
  transfers between devices with their start and end apart: 7, of which 7 were waited for; matrix products, arithmetic and copies ran while one was open for 4% of the time, Pallas kernels for 0%

commit v1 on v0

v1 whole, which is shorter than its diff:
```python
from fractions import Fraction

import jax
import jax.numpy as jnp
from jax import lax
from jax.experimental import pallas as pl
from jax.experimental.pallas import tpu as pltpu
from jax.sharding import PartitionSpec as P

ALL = ("grp", "dev")

TABLEAU = (
    ("1/5",),
    ("3/40", "9/40"),
    ("44/45", "-56/15", "32/9"),
    ("19372/6561", "-25360/2187", "64448/6561", "-212/729"),
    ("9017/3168", "-355/33", "46732/5247", "49/176", "-5103/18656"),
    ("35/384", "0", "500/1113", "125/192", "-2187/6784", "11/84"),
)
ERRORS = ("71/57600", "0", "-71/16695", "71/1920", "-17253/339200", "22/525", "-1/40")
ABS_TOL = 0.001
REL_TOL = 0.01
UNIT_STEP = 1.0 / 64

N = 24
LINKS = 8
SLOT = 2
USES = 4
LANES = 128
SQ = N * N
ROWS = 2 * SQ
LINE = 4 * N
PIECES = SLOT * USES
FEATURES = PIECES * LINE
BLOCKS = FEATURES // LANES
COUPLINGS = LINKS * LANES
HIGHEST = lax.Precision.HIGHEST
F32 = jnp.float32
BF16 = jnp.bfloat16


def step_polynomials():
    def axpy(left, weight, right):
        size = max(len(left), len(right))
        left = left + [Fraction(0)] * (size - len(left))
        right = right + [Fraction(0)] * (size - len(right))
        return [a + weight * b for a, b in zip(left, right)]

    inner = [Fraction(1)]
    sections = [[Fraction(0)] + inner]
    for weights in TABLEAU:
        inner = [Fraction(1)]
        for weight, section in zip(weights, sections):
            inner = axpy(inner, Fraction(weight), section)
        sections.append([Fraction(0)] + inner)
    error = [Fraction(0)]
    for weight, section in zip(ERRORS, sections):
        error = axpy(error, Fraction(weight), section)
    return [float(x) for x in inner], [float(x) for x in error]


NEW, ERR = step_polynomials()
POWERS = len(ERR) - 1


def split(x):
    high = x.astype(BF16)
    low = (x - high.astype(F32)).astype(BF16)
    return high, low


def dot(a, b, **kw):
    return jnp.dot(a, b, preferred_element_type=F32, **kw)


def div24(x):
    return lax.shift_right_logical(x * 2731, 16)


def call(body, outs, scratch=(), flops=1000000, name=None, smem=(), args=()):
    specs = [
        pl.BlockSpec(memory_space=pltpu.SMEM if i in smem else pltpu.VMEM) for i in range(len(args))
    ]
    return pl.pallas_call(
        body,
        out_shape=[jax.ShapeDtypeStruct(s, d) for s, d in outs],
        in_specs=specs,
        out_specs=[pl.BlockSpec(memory_space=pltpu.VMEM) for _ in outs],
        scratch_shapes=[pltpu.VMEM(s, d) for s, d in scratch],
        compiler_params=pltpu.CompilerParams(vmem_limit_bytes=24 * 1024 * 1024),
        cost_estimate=pl.CostEstimate(flops=flops, bytes_accessed=4000000, transcendentals=0),
        name=name,
    )(*args)


def plan_body(src_ref, site_ref, place_ref, ask_ref):
    src = src_ref[...]
    srcf = src.astype(F32)
    turned = jnp.concatenate([srcf, jnp.zeros((LANES - LINKS, LANES), F32)], axis=0).T
    sub = lax.broadcasted_iota(jnp.int32, (LANES, LANES), 0)
    lane = lax.broadcasted_iota(jnp.int32, (LANES, LANES), 1)
    deep = lax.broadcasted_iota(jnp.int32, (COUPLINGS, LANES), 0)
    piece_row = lax.broadcasted_iota(jnp.int32, (PIECES, LANES), 0)
    asked = jnp.zeros((LANES, PIECES), F32)
    for l in range(LINKS):
        mine = jnp.broadcast_to(srcf[l : l + 1, :], (LANES, LANES))
        same = jnp.zeros((LANES, LANES), F32)
        for q in range(l + 1):
            other = jnp.broadcast_to(turned[:, q : q + 1], (LANES, LANES))
            hit = other == mine
            if q == l:
                hit = hit & (sub < lane)
            same = same + jnp.where(hit, 1.0, 0.0)
        rank = jnp.sum(same, axis=0, keepdims=True).astype(jnp.int32)
        place = src[l : l + 1, :] - LANES
        slot = lax.bitwise_and(place, SLOT - 1)
        owner = lax.shift_right_arithmetic(place, 1)
        index = jnp.where(place >= 0, (slot * USES + rank) * LANES + owner, -1)
        hot = jnp.where(deep == jnp.broadcast_to(index, (COUPLINGS, LANES)), 1.0, 0.0).astype(BF16)
        place_ref[:, l * LANES : (l + 1) * LANES] = hot
        owned = jnp.where(sub == owner, 1.0, 0.0).astype(BF16)
        wanted = jnp.where(
            (piece_row == slot * USES + rank) & (place >= 0), site_ref[l : l + 1, :].astype(F32), 0.0
        ).astype(BF16)
        asked = asked + lax.dot_general(
            owned, wanted, (((1,), (1,)), ((), ())), preferred_element_type=F32
        )
    ask_ref[...] = jnp.zeros((LANES, LANES), F32)
    ask_ref[:, 0:PIECES] = asked


def tables_body(
    units_ref, ham_ref, rates_ref, modes_ref, src_ref, coef_ref, send_ref,
    high_ref, low_ref, decay_ref, own_ref, pick_ref, scaled_ref,
):
    h = units_ref[0].astype(F32) * UNIT_STEP
    ham = ham_ref[...]
    row = lax.broadcasted_iota(jnp.int32, (N, N), 0)
    column = lax.broadcasted_iota(jnp.int32, (N, N), 1)
    unit = jnp.where(row == column, 1.0, 0.0)
    flipped = lax.dot_general(
        unit, ham, (((1,), (1,)), ((), ())), precision=HIGHEST, preferred_element_type=F32
    )
    sym = h * (0.5 * (ham + flipped))
    at = lax.broadcasted_iota(jnp.int32, (N, SQ), 1)
    row = lax.broadcasted_iota(jnp.int32, (N, SQ), 0)
    first = div24(at)
    same_second = row == at - first * N
    by_first = dot(sym, jnp.where(row == first, 1.0, 0.0), precision=HIGHEST)
    by_second = dot(sym, jnp.where(same_second, 1.0, 0.0), precision=HIGHEST)
    for a in range(N):
        block = jnp.where(same_second, jnp.broadcast_to(by_first[a : a + 1, :], (N, SQ)), 0.0)
        high, low = split(block - jnp.where(first == a, by_second, 0.0))
        high_ref[a * N : (a + 1) * N, :] = high
        low_ref[a * N : (a + 1) * N, :] = low
    level = lax.broadcasted_iota(jnp.int32, (rates_ref.shape[1], LANES), 0)
    hits = jnp.zeros((rates_ref.shape[1], LANES), F32)
    for m in range(modes_ref.shape[0]):
        hits = hits + jnp.where(level == modes_ref[m : m + 1, :], 1.0, 0.0)
    rates = jnp.broadcast_to(rates_ref[...], (8, rates_ref.shape[1]))
    decay_ref[...] = h * dot(rates, hits, precision=HIGHEST)
    sub = lax.broadcasted_iota(jnp.int32, (LANES, LANES), 0)
    for l in range(LINKS):
        hot = jnp.where(sub == src_ref[l : l + 1, :], 1.0, 0.0).astype(BF16)
        own_ref[l, 0:LANES, :] = hot
        own_ref[l, LANES : 2 * LANES, :] = hot
    wide = SLOT * LANES
    i = lax.broadcasted_iota(jnp.int32, (wide, wide), 0)
    p = lax.broadcasted_iota(jnp.int32, (wide, wide), 1)
    order = jnp.where(
        i == lax.bitwise_and(p, LANES - 1) * SLOT + lax.shift_right_logical(p, 7), 1.0, 0.0
    ).astype(BF16)
    ids = jnp.broadcast_to(send_ref[...].astype(F32), (8, wide)).astype(BF16)
    sorted_ids = dot(ids, order)[0:1, :].astype(jnp.int32)
    sub = lax.broadcasted_iota(jnp.int32, (LANES, wide), 0)
    hot = jnp.where(sub == sorted_ids, 1.0, 0.0).astype(BF16)
    pick_ref[0:LANES, :] = hot
    pick_ref[LANES : 2 * LANES, :] = hot
    scaled_ref[...] = h * coef_ref[...]


def lines(read_row, read_column, sites, store):
    for kind, read in ((0, read_row), (1, read_column)):
        kept = [[[None] * 3 for _ in range(2)] for _ in sites]
        for k in range(N):
            tile = [[read(c, k, t) for t in range(3)] for c in range(2)]
            for u, site in enumerate(sites):
                hit = site == k if k else None
                for c in range(2):
                    for t in range(3):
                        kept[u][c][t] = (
                            jnp.where(hit, tile[c][t], kept[u][c][t]) if k else tile[c][t]
                        )
        for u in range(len(sites)):
            for c in range(2):
                for t in range(3):
                    store(u, kind * 2 * N + c * N + t * 8, kept[u][c][t])


def local_part(v_ref, high_ref, low_ref, decay_ref, own_ref, site_ref, base, line, both_ref, even, odd):
    real, imag = v_ref[0:SQ, :], v_ref[SQ:ROWS, :]
    real_high, real_low = split(real)
    imag_high, imag_low = split(imag)
    high = jnp.concatenate([real_high, imag_high], axis=0)
    low = jnp.concatenate([real_low, imag_low], axis=0)
    both_ref[...] = jnp.concatenate([high, low], axis=1)

    def fetch(l, place):
        place[...] = dot(both_ref[...], own_ref[l])

    def pick(l, place):
        site = jnp.broadcast_to(site_ref[pl.ds(l, 1), :], (8, LANES))

        def store(u, f, value):
            line[l, f : f + 8, :] = value

        lines(
            lambda c, k, t: place[pl.ds(c * SQ + k * N + t * 8, 8), :],
            lambda c, k, t: place[pl.ds(c * SQ + t * 8 * N + k, 8, stride=N), :],
            [site],
            store,
        )

    def pair(i, carry):
        fetch(2 * i + 1, odd)
        pick(2 * i, even)
        fetch(jnp.minimum(2 * i + 2, LINKS - 1), even)
        pick(2 * i + 1, odd)
        return carry

    fetch(0, even)
    lax.fori_loop(0, LINKS // 2, pair, 0)
    x_high = jnp.concatenate([real_high, imag_high], axis=1)
    x_low = jnp.concatenate([real_low, imag_low], axis=1)
    turned = dot(high_ref[...], x_high) + dot(high_ref[...], x_low) + dot(low_ref[...], x_high)
    decay = jnp.broadcast_to(decay_ref[0:1, :], (SQ, LANES))
    base[0:SQ, :] = turned[:, LANES:] - decay * real
    base[SQ:ROWS, :] = -turned[:, :LANES] - decay * imag


def pack_part(v_ref, pick_ref, sites, send_ref, full, feats):
    high, low = split(v_ref[...])
    picked = dot(jnp.concatenate([high, low], axis=1), pick_ref[...])
    for s in range(SLOT):
        full[s] = picked[:, s * LANES : (s + 1) * LANES]
    for s in range(SLOT):
        wanted = [
            jnp.broadcast_to(sites[s * USES + u : s * USES + u + 1, :], (8, LANES))
            for u in range(USES)
        ]

        def store(u, f, value):
            row = (s * USES + u) * LINE + f
            feats[row : row + 8, :] = value

        lines(
            lambda c, k, t: full[s, pl.ds(c * SQ + k * N + t * 8, 8), :],
            lambda c, k, t: full[s, pl.ds(c * SQ + t * 8 * N + k, 8, stride=N), :],
            wanted,
            store,
        )
    for k in range(BLOCKS):
        send_ref[pl.ds(k, LANES, stride=BLOCKS), :] = feats[k * LANES : (k + 1) * LANES, :].T


def first_pack(v, pick, asked):
    def body(v_ref, pick_ref, asked_ref, send_ref, want_ref, full, feats):
        want = asked_ref[...].T[0:PIECES, :].astype(jnp.int32)
        want_ref[...] = want
        pack_part(v_ref, pick_ref, want, send_ref, full, feats)

    return call(
        body,
        [((BLOCKS * LANES, LANES), F32), ((PIECES, LANES), jnp.int32)],
        [((SLOT, ROWS, LANES), F32), ((FEATURES, LANES), F32)],
        flops=10**8, name="pack_first", args=(v, pick, asked),
    )


def gather_part(got_ref, place_ref, site_ref, coef_ref, base_ref, line_ref, emit, feats, cols):
    for k in range(BLOCKS):
        feats[k * LANES : (k + 1) * LANES, :] = got_ref[pl.ds(k, LANES, stride=BLOCKS), :].T
    wide = jnp.concatenate([feats[p * LINE : (p + 1) * LINE, :] for p in range(PIECES)], axis=1)
    high, low = split(wide)
    both = dot(jnp.concatenate([high, low], axis=0), place_ref[...])
    found = both[0:LINE, :] + both[LINE:, :]
    sites = [jnp.broadcast_to(site_ref[l : l + 1, :], (8, LANES)) for l in range(LINKS)]

    def term(kind, c, l):
        rows = slice(kind * 2 * N, (kind + 1) * 2 * N)
        x = found[rows, l * LANES : (l + 1) * LANES] + line_ref[l, rows, :]
        re, im = x[0:N], x[N:]
        row = 2 * kind * LINKS + l
        cr = jnp.broadcast_to(coef_ref[row : row + 1, :], (N, LANES))
        ci = jnp.broadcast_to(coef_ref[row + LINKS : row + LINKS + 1, :], (N, LANES))
        value = cr * im + ci * re if c == 0 else ci * im - cr * re
        return -value if kind else value

    for kind in (1, 0):
        for c in range(2):
            terms = [term(kind, c, l) for l in range(LINKS)]
            for k in range(N):
                hits = [site == k for site in sites]
                for t in range(3):
                    if kind:
                        total = jnp.zeros((8, LANES), F32)
                    else:
                        at = c * SQ + k * N + t * 8
                        total = base_ref[at : at + 8, :]
                        total = total + cols[pl.ds(c * SQ + t * 8 * N + k, 8, stride=N), :]
                    for l in range(LINKS):
                        total = total + jnp.where(hits[l], terms[l][t * 8 : t * 8 + 8], 0.0)
                    if kind:
                        at = c * SQ + k * N + t * 8
                        cols[at : at + 8, :] = total
                    else:
                        emit(at, total)


SCRATCH = [
    ((ROWS, LANES), F32),
    ((LINKS, LINE, LANES), F32),
    ((ROWS, 2 * LANES), BF16),
    ((SLOT, ROWS, LANES), F32),
    ((FEATURES, LANES), F32),
    ((ROWS, LANES), F32),
]


def advance(weight, got, v, total, tables, site, want):
    def body(got_ref, v_ref, total_ref, place_ref, high_ref, low_ref, decay_ref, own_ref, pick_ref,
             coef_ref, site_ref, want_ref, next_ref, send_ref, sum_ref, base, line, both, full, feats, cols):
        local_part(v_ref, high_ref, low_ref, decay_ref, own_ref, site_ref, base, line, both, full.at[0], full.at[1])

        def emit(at, value):
            next_ref[at : at + 8, :] = value
            sum_ref[at : at + 8, :] = total_ref[at : at + 8, :] + weight * value

        gather_part(got_ref, place_ref, site_ref, coef_ref, base, line, emit, feats, cols)
        pack_part(next_ref, pick_ref, want_ref[...], send_ref, full, feats)

    return call(
        body,
        [((ROWS, LANES), F32), ((BLOCKS * LANES, LANES), F32), ((ROWS, LANES), F32)],
        SCRATCH, name="advance", args=(got, v, total, *tables, site, want),
    )


def finish(got, v, before, state, new, tables, site):
    def body(got_ref, v_ref, before_ref, state_ref, new_ref, place_ref, high_ref, low_ref, decay_ref,
             own_ref, pick_ref, coef_ref, site_ref, out_ref, base, line, both, full, feats, cols, sums):
        local_part(v_ref, high_ref, low_ref, decay_ref, own_ref, site_ref, base, line, both, full.at[0], full.at[1])
        sums[...] = jnp.zeros((8, LANES), F32)

        def emit(at, value):
            rows = slice(at, at + 8)
            error = (
                ERR[POWERS - 2] * before_ref[rows, :]
                + ERR[POWERS - 1] * v_ref[rows, :]
                + ERR[POWERS] * value
            )
            largest = jnp.maximum(jnp.abs(state_ref[rows, :]), jnp.abs(new_ref[rows, :]))
            scaled = error / (ABS_TOL + REL_TOL * largest)
            sums[...] = sums[...] + scaled * scaled

        gather_part(got_ref, place_ref, site_ref, coef_ref, base, line, emit, feats, cols)
        out_ref[...] = jnp.broadcast_to(jnp.sum(sums[...], axis=0, keepdims=True), (LANES, LANES))

    (out,) = call(
        body,
        [((LANES, LANES), F32)],
        SCRATCH + [((8, LANES), F32)],
        name="finish", args=(got, v, before, state, new, *tables, site),
    )
    return out


def exchange(x):
    peers = LANES
    flat = x.reshape(peers, 1, x.size // peers)
    moved = lax.all_to_all(flat, ALL, split_axis=0, concat_axis=0, tiled=True)
    return moved.reshape(x.shape)


def shards(
    state, hamiltonian, mode_rates, ado_modes, link_src, link_site, link_coef, send_ids, step_units
):
    v = state.reshape(ROWS, LANES)
    place, ask = call(
        plan_body,
        [((COUPLINGS, COUPLINGS), BF16), ((LANES, LANES), F32)],
        flops=10**8, name="plan", args=(link_src, link_site),
    )
    asked = exchange(ask)
    high, low, decay, own, pick, coef = call(
        tables_body,
        [
            ((SQ, SQ), BF16),
            ((SQ, SQ), BF16),
            ((8, LANES), F32),
            ((LINKS, 2 * LANES, LANES), BF16),
            ((2 * LANES, SLOT * LANES), BF16),
            ((4 * LINKS, LANES), F32),
        ],
        flops=10**9, name="tables", smem=(0,),
        args=(
            step_units.reshape(1), hamiltonian, mode_rates.reshape(1, -1), ado_modes, link_src,
            link_coef.reshape(4 * LINKS, LANES), send_ids,
        ),
    )
    send, want = first_pack(v, pick, asked)
    total, before = v, v
    tables = (place, high, low, decay, own, pick, coef)
    for n in range(1, POWERS):
        before = v
        v, send, total = advance(NEW[n], exchange(send), before, total, tables, link_site, want)
    start = state.reshape(ROWS, LANES)
    sums = exchange(finish(exchange(send), v, before, start, total, tables, link_site))
    entries = state.size * lax.axis_size(ALL)
    return total.reshape(state.shape), jnp.sqrt(jnp.sum(sums) / entries)


def solution(mesh):
    return jax.shard_map(
        shards,
        mesh=mesh,
        in_specs=(
            P(None, None, None, ALL),
            P(),
            P(),
            P(None, ALL),
            P(None, ALL),
            P(None, ALL),
            P(None, None, ALL),
            P(ALL, None),
            P(),
        ),
        out_specs=(P(None, None, None, ALL), P()),
        check_vma=False,
    )
```

time: 509 us -> 201 us (0.39)
  local copies, waits for them, and re-layouts: 194 us -> 8.57 us
  waiting for transfers between devices: 111 us -> 2.6 us
  blocking collectives: 32.6 us -> 131 us
  other arithmetic: 59.6 us -> 0.73 us
  matrix products: 50.3 us -> 0 us
  Pallas kernels: 0 us -> 41.1 us
  starting transfers between devices: 49.4 us -> 11.7 us
    all_to_all x0 -> x8, blocking collectives: none -> 131 us  [exchange(): moved = lax.all_to_all(flat, ALL, split_axis=0, concat_axis=0, tiled=True)]
    all_to_all x7 -> x1, waiting for transfers between devices: 111 us -> 2.6 us  [exchange(): moved = lax.all_to_all(flat, ALL, split_axis=0, concat_axis=0, tiled=True)]
    unnamed x550 -> x26, local copies, waits for them, and re-layouts: 107 us -> 8.57 us
    dot_general x28 -> x0, matrix products: 50.3 us -> none  [the longest x7 32.2 us: evaluate(): fetched = jnp.dot(combined, link_table, precision=HIGHEST)]
    pallas_call x0 -> x10, Pallas kernels: none -> 41.1 us  [call(): pl.pallas_call(body, out_shape=[jax.ShapeDtypeStruct(s, d) for s, d in ou...]
    all_to_all x8 -> x0, local copies, waits for them, and re-layouts: 40.2 us -> none  [evaluate(): lax.all_to_all(packed, GRP_DEV, split_axis=3, concat_axis=3, tiled=True)]
    all_to_all x7 -> x1, starting transfers between devices: 49.4 us -> 11.7 us  [exchange(): moved = lax.all_to_all(flat, ALL, split_axis=0, concat_axis=0, tiled=True)]
    dot_general x7 -> x0, local copies, waits for them, and re-layouts: 35.6 us -> none  [evaluate(): jnp.dot(flat_current, pack_table, precision=HIGHEST)]
  transfers between devices with their start and end apart: 7 -> 1, of which waited for: 7 -> 1; matrix products, arithmetic and copies ran while one was open for 4% -> 0% of each run, Pallas kernels for 0% -> 0%
where the time goes in v1:
time: 201 us; the launch traced here: 199 us
  blocking collectives  131 us (65%)
  Pallas kernels  41.1 us (20%)
  starting transfers between devices  11.7 us (6%)
  local copies, waits for them, and re-layouts  8.57 us (4%)
  between operations  3.19 us (2%)
  waiting for transfers between devices  2.6 us (1%)
    all_to_all x8, blocking collectives, exchange(): moved = lax.all_to_all(flat, ALL, split_axis=0, concat_axis=0, tiled=True)  131 us
    pallas_call x10, Pallas kernels, call(): pl.pallas_call(body, out_shape=[jax.ShapeDtypeStruct(s, d) for s, d in ou...  41.1 us
    all_to_all x1, starting transfers between devices, exchange(): moved = lax.all_to_all(flat, ALL, split_axis=0, concat_axis=0, tiled=True)  11.7 us
    unnamed x26, local copies, waits for them, and re-layouts  8.57 us
  transfers between devices with their start and end apart: 1, of which 1 were waited for; matrix products, arithmetic and copies ran while one was open for 0% of the time, Pallas kernels for 0%

profile of v1, /device:TPU:0, one launch (start us, length us, event | category | flops | bytes accessed | tf_op | source)
XLA Modules:
  0.0 199.4 jit_solution(12233980717855064367)
XLA Ops:
  0.6 0.7 copy-done.4
  1.3 0.7 copy-done.8
  2.0 2.4 %plan.1 = (bf16[1024,1024]{1,0:T(8,128)(2,1)S(1)}, f32[128,128]{1,0:T(8,128)}) custom-call(s32[8,128]{1,0:T(8,128)S(1)} %copy-done.8, s32[8,128]{1,0:T(8,128)S(1)} %copy-done.4), custom_call_target="tpu_custom_call" | custom-call | flops 100000000 | bytes 4000000 | tf_op jit(solution)/shard_map/plan/pallas_call | solution.py:84
  4.4 11.7 %all-to-all-start = ((f32[128,1,128]{2,1,0:T(1,128)}), f32[128,1,128]{2,1,0:T(1,128)}, u32[]{:S(2)}, u32[]{:S(2)}) async-start(f32[128,1,128]{2,1,0:T(1,128)} %bitcast.5), calls=%async_computation | async-start | bytes 131072 | tf_op jit(solution)/shard_map/all_to_all | solution.py:381
  16.7 0.7 copy-done.6
  17.5 0.7 copy-done.7
  18.2 0.7 copy-done.9
  18.9 0.7 copy-done.10
  19.5 0.7 copy-done.11
  20.2 0.7 copy-done.12
  20.9 0.8 tables.1
  21.7 0.9 copy-done
  22.5 2.6 %all-to-all-done = f32[128,1,128]{2,1,0:T(1,128)} async-done(((f32[128,1,128]{2,1,0:T(1,128)}), f32[128,1,128]{2,1,0:T(1,128)}, u32[]{:S(2)}, u32[]{:S(2)}) %all-to-all-start) | async-done | bytes 65568 | tf_op jit(solution)/shard_map/all_to_all | solution.py:381
  25.1 1.1 copy-done.2
  26.3 1.7 pack_first.1
  28.0 18.5 %all_to_all.45 = f32[128,1,768]{2,1,0:T(1,128)S(1)} all-to-all(f32[128,1,768]{2,1,0:T(1,128)S(1)} %bitcast.45), channel_id=1, replica_groups=mesh['grp'=2,'dev'=64] {'grp','dev'}, dimensions={0} | all-to-all | bytes 786432 | tf_op jit(solution)/shard_map/all_to_all | solution.py:381
  46.5 5.2 %advance.6 = (f32[1152,128]{1,0:T(8,128)S(1)}, f32[768,128]{1,0:T(8,128)S(1)}, f32[1152,128]{1,0:T(8,128)S(1)}) custom-call(f32[768,128]{1,0:T(8,128)S(1)} %bitcast.31, f32[1152,128]{1,0:T(8,128)S(1)} %bitcast.28, f32[1152,128]{1,0:T(8,128)S(1)} %bitcast.29, bf16[1024,1024]{1,0:T(8,128)(2,1)S(1)} %get-tuple-element.33.place_ref, ...), custom_call_target="tpu_custom_call" | custom-call | flops 1000000 | bytes 4000000 | tf_op jit(solution)/shard_map/advance/pallas_call | solution.py:84
  51.7 16.5 %all_to_all.46 = f32[128,1,768]{2,1,0:T(1,128)S(1)} all-to-all(f32[128,1,768]{2,1,0:T(1,128)S(1)} %bitcast.44), channel_id=1, replica_groups=mesh['grp'=2,'dev'=64] {'grp','dev'}, dimensions={0} | all-to-all | bytes 786432 | tf_op jit(solution)/shard_map/all_to_all | solution.py:381
  68.2 5.3 %advance.7 = (f32[1152,128]{1,0:T(8,128)S(1)}, f32[768,128]{1,0:T(8,128)S(1)}, f32[1152,128]{1,0:T(8,128)S(1)}) custom-call(f32[768,128]{1,0:T(8,128)S(1)} %bitcast.32, f32[1152,128]{1,0:T(8,128)S(1)} %get-tuple-element.41.v_ref, f32[1152,128]{1,0:T(8,128)S(1)} %get-tuple-element.42.total_ref, bf16[1024,1024]{1,0:T(8,128)(2,1)S(1)} %get-tuple-element.33.place_ref, ...), custom_call_target="tpu_custom_call" | custom-call | flops 1000000 | bytes 4000000 | tf_op jit(solution)/shard_map/advance/pallas_call | solution.py:84
  73.5 16.5 %all_to_all.47 = f32[128,1,768]{2,1,0:T(1,128)S(1)} all-to-all(f32[128,1,768]{2,1,0:T(1,128)S(1)} %bitcast.39), channel_id=1, replica_groups=mesh['grp'=2,'dev'=64] {'grp','dev'}, dimensions={0} | all-to-all | bytes 786432 | tf_op jit(solution)/shard_map/all_to_all | solution.py:381
  90.0 5.2 %advance.8 = (f32[1152,128]{1,0:T(8,128)S(1)}, f32[768,128]{1,0:T(8,128)S(1)}, f32[1152,128]{1,0:T(8,128)S(1)}) custom-call(f32[768,128]{1,0:T(8,128)S(1)} %bitcast.33, f32[1152,128]{1,0:T(8,128)S(1)} %get-tuple-element.44.v_ref, f32[1152,128]{1,0:T(8,128)S(1)} %get-tuple-element.45.total_ref, bf16[1024,1024]{1,0:T(8,128)(2,1)S(1)} %get-tuple-element.33.place_ref, ...), custom_call_target="tpu_custom_call" | custom-call | flops 1000000 | bytes 4000000 | tf_op jit(solution)/shard_map/advance/pallas_call | solution.py:84
  95.2 16.5 %all_to_all.48 = f32[128,1,768]{2,1,0:T(1,128)S(1)} all-to-all(f32[128,1,768]{2,1,0:T(1,128)S(1)} %bitcast.40), channel_id=1, replica_groups=mesh['grp'=2,'dev'=64] {'grp','dev'}, dimensions={0} | all-to-all | bytes 786432 | tf_op jit(solution)/shard_map/all_to_all | solution.py:381
  111.7 5.3 %advance.9 = (f32[1152,128]{1,0:T(8,128)S(1)}, f32[768,128]{1,0:T(8,128)S(1)}, f32[1152,128]{1,0:T(8,128)S(1)}) custom-call(f32[768,128]{1,0:T(8,128)S(1)} %bitcast.34, f32[1152,128]{1,0:T(8,128)S(1)} %get-tuple-element.47.v_ref, f32[1152,128]{1,0:T(8,128)S(1)} %get-tuple-element.48.total_ref, bf16[1024,1024]{1,0:T(8,128)(2,1)S(1)} %get-tuple-element.33.place_ref, ...), custom_call_target="tpu_custom_call" | custom-call | flops 1000000 | bytes 4000000 | tf_op jit(solution)/shard_map/advance/pallas_call | solution.py:84
  116.9 16.5 %all_to_all.49 = f32[128,1,768]{2,1,0:T(1,128)S(1)} all-to-all(f32[128,1,768]{2,1,0:T(1,128)S(1)} %bitcast.41), channel_id=1, replica_groups=mesh['grp'=2,'dev'=64] {'grp','dev'}, dimensions={0} | all-to-all | bytes 786432 | tf_op jit(solution)/shard_map/all_to_all | solution.py:381
  133.4 5.3 %advance.10 = (f32[1152,128]{1,0:T(8,128)S(1)}, f32[768,128]{1,0:T(8,128)S(1)}, f32[1152,128]{1,0:T(8,128)S(1)}) custom-call(f32[768,128]{1,0:T(8,128)S(1)} %bitcast.35, f32[1152,128]{1,0:T(8,128)S(1)} %get-tuple-element.50.v_ref, f32[1152,128]{1,0:T(8,128)S(1)} %get-tuple-element.51.total_ref, bf16[1024,1024]{1,0:T(8,128)(2,1)S(1)} %get-tuple-element.33.place_ref, ...), custom_call_target="tpu_custom_call" | custom-call | flops 1000000 | bytes 4000000 | tf_op jit(solution)/shard_map/advance/pallas_call | solution.py:84
  138.7 16.5 %all_to_all.50 = f32[128,1,768]{2,1,0:T(1,128)S(1)} all-to-all(f32[128,1,768]{2,1,0:T(1,128)S(1)} %bitcast.42), channel_id=1, replica_groups=mesh['grp'=2,'dev'=64] {'grp','dev'}, dimensions={0} | all-to-all | bytes 786432 | tf_op jit(solution)/shard_map/all_to_all | solution.py:381
  155.2 5.5 %advance.11 = (f32[1152,128]{1,0:T(8,128)S(1)}, f32[768,128]{1,0:T(8,128)S(1)}, f32[1152,128]{1,0:T(8,128)}) custom-call(f32[768,128]{1,0:T(8,128)S(1)} %bitcast.36, f32[1152,128]{1,0:T(8,128)S(1)} %get-tuple-element.53.v_ref.before_ref, f32[1152,128]{1,0:T(8,128)S(1)} %get-tuple-element.54.total_ref, bf16[1024,1024]{1,0:T(8,128)(2,1)S(1)} %get-tuple-element.33.place_ref, ...), custom_call_target="tpu_custom_call" | custom-call | flops 1000000 | bytes 4000000 | tf_op jit(solution)/shard_map/advance/pallas_call | solution.py:84
  160.7 16.5 %all_to_all.51 = f32[128,1,768]{2,1,0:T(1,128)S(1)} all-to-all(f32[128,1,768]{2,1,0:T(1,128)S(1)} %bitcast.43), channel_id=1, replica_groups=mesh['grp'=2,'dev'=64] {'grp','dev'}, dimensions={0} | all-to-all | bytes 786432 | tf_op jit(solution)/shard_map/all_to_all | solution.py:381
  177.2 1.1 copy-done.3
  178.3 4.5 %finish.1 = f32[128,128]{1,0:T(8,128)S(1)} custom-call(f32[768,128]{1,0:T(8,128)S(1)} %bitcast.37, f32[1152,128]{1,0:T(8,128)S(1)} %get-tuple-element.57.v_ref, f32[1152,128]{1,0:T(8,128)S(1)} %get-tuple-element.53.v_ref.before_ref, f32[1152,128]{1,0:T(8,128)S(1)} %bitcast.30, f32[1152,128]{1,0:T(8,128)S(1)} %copy-done.3, ...), custom_call_target="tpu_custom_call" | custom-call | flops 1000000 | bytes 4000000 | tf_op jit(solution)/shard_map/finish/pallas_call | solution.py:84
  182.8 14.0 %all_to_all.52 = f32[128,1,128]{2,1,0:T(1,128)S(1)} all-to-all(f32[128,1,128]{2,1,0:T(1,128)S(1)} %bitcast.46), channel_id=1, replica_groups=mesh['grp'=2,'dev'=64] {'grp','dev'}, dimensions={0} | all-to-all | bytes 131072 | tf_op jit(solution)/shard_map/all_to_all | solution.py:381
  196.8 0.7 reduce_sum.9
  (15 shorter events, 0.0 us)
Async XLA Ops:
  0.6 0.7 copy-start.4
  1.3 0.7 copy-start.8
  4.4 20.8 %all-to-all-start = ((f32[128,1,128]{2,1,0:T(1,128)}), f32[128,1,128]{2,1,0:T(1,128)}, u32[]{:S(2)}, u32[]{:S(2)}) async-start(f32[128,1,128]{2,1,0:T(1,128)} %bitcast.5), calls=%async_computation | async-start | bytes 131072 | tf_op jit(solution)/shard_map/all_to_all | solution.py:381
  16.7 0.7 copy-start.6
  17.5 0.7 copy-start.7
  18.2 0.7 copy-start.9
  18.8 0.7 copy-start.10
  19.5 0.7 copy-start.11
  20.2 0.7 copy-start.12
  20.9 25.6 %copy-start.5 = (s32[8,128]{1,0:T(8,128)S(1)}, s32[8,128]{1,0:T(8,128)}, u32[]{:S(2)}) copy-start(s32[8,128]{1,0:T(8,128)} %site_ref.15) | copy-start | bytes 12292
  21.7 0.9 copy-start
  25.1 21.4 %copy-start.1 = (bf16[576,576]{1,0:T(8,128)(2,1)S(1)}, bf16[576,576]{1,0:T(8,128)(2,1)}, u32[]{:S(2)}) copy-start(bf16[576,576]{1,0:T(8,128)(2,1)} %copy-done) | copy-start | bytes 1990660
  25.1 1.1 copy-start.2
  177.2 1.1 copy-start.3

commit v2 on v1

--- a/solution.py
+++ b/solution.py
@@ -77,7 +77,7 @@
     return lax.shift_right_logical(x * 2731, 16)
 
 
-def call(body, outs, scratch=(), flops=1000000, name=None, smem=(), args=()):
+def call(body, outs, scratch=(), flops=1000000, name=None, smem=(), args=(), aliases=None):
     specs = [
         pl.BlockSpec(memory_space=pltpu.SMEM if i in smem else pltpu.VMEM) for i in range(len(args))
     ]
@@ -89,17 +89,17 @@
         scratch_shapes=[pltpu.VMEM(s, d) for s, d in scratch],
         compiler_params=pltpu.CompilerParams(vmem_limit_bytes=24 * 1024 * 1024),
         cost_estimate=pl.CostEstimate(flops=flops, bytes_accessed=4000000, transcendentals=0),
+        input_output_aliases=aliases or {},
         name=name,
     )(*args)
 
 
-def plan_body(src_ref, site_ref, place_ref, ask_ref):
+def plan_body(src_ref, site_ref, place_ref, piece_ref, ask_ref):
     src = src_ref[...]
     srcf = src.astype(F32)
     turned = jnp.concatenate([srcf, jnp.zeros((LANES - LINKS, LANES), F32)], axis=0).T
     sub = lax.broadcasted_iota(jnp.int32, (LANES, LANES), 0)
     lane = lax.broadcasted_iota(jnp.int32, (LANES, LANES), 1)
-    deep = lax.broadcasted_iota(jnp.int32, (COUPLINGS, LANES), 0)
     piece_row = lax.broadcasted_iota(jnp.int32, (PIECES, LANES), 0)
     asked = jnp.zeros((LANES, PIECES), F32)
     for l in range(LINKS):
@@ -115,12 +115,13 @@
         place = src[l : l + 1, :] - LANES
         slot = lax.bitwise_and(place, SLOT - 1)
         owner = lax.shift_right_arithmetic(place, 1)
-        index = jnp.where(place >= 0, (slot * USES + rank) * LANES + owner, -1)
-        hot = jnp.where(deep == jnp.broadcast_to(index, (COUPLINGS, LANES)), 1.0, 0.0).astype(BF16)
-        place_ref[:, l * LANES : (l + 1) * LANES] = hot
+        piece = jnp.where(place >= 0, slot * USES + rank, -1)
+        piece_ref[l : l + 1, :] = piece
         owned = jnp.where(sub == owner, 1.0, 0.0).astype(BF16)
+        place_ref[0:LANES, l * LANES : (l + 1) * LANES] = owned
+        place_ref[LANES : 2 * LANES, l * LANES : (l + 1) * LANES] = owned
         wanted = jnp.where(
-            (piece_row == slot * USES + rank) & (place >= 0), site_ref[l : l + 1, :].astype(F32), 0.0
+            piece_row == piece, site_ref[l : l + 1, :].astype(F32), 0.0
         ).astype(BF16)
         asked = asked + lax.dot_general(
             owned, wanted, (((1,), (1,)), ((), ())), preferred_element_type=F32
@@ -130,8 +131,8 @@
 
 
 def tables_body(
-    units_ref, ham_ref, rates_ref, modes_ref, src_ref, coef_ref, send_ref,
-    high_ref, low_ref, decay_ref, own_ref, pick_ref, scaled_ref,
+    units_ref, ham_ref, rates_ref, modes_ref, coef_ref, send_ref,
+    first_ref, second_ref, decay_ref, pick_ref, scaled_ref,
 ):
     h = units_ref[0].astype(F32) * UNIT_STEP
     ham = ham_ref[...]
@@ -148,22 +149,14 @@
     same_second = row == at - first * N
     by_first = dot(sym, jnp.where(row == first, 1.0, 0.0), precision=HIGHEST)
     by_second = dot(sym, jnp.where(same_second, 1.0, 0.0), precision=HIGHEST)
-    for a in range(N):
-        block = jnp.where(same_second, jnp.broadcast_to(by_first[a : a + 1, :], (N, SQ)), 0.0)
-        high, low = split(block - jnp.where(first == a, by_second, 0.0))
-        high_ref[a * N : (a + 1) * N, :] = high
-        low_ref[a * N : (a + 1) * N, :] = low
+    first_ref[...] = by_first
+    second_ref[...] = by_second
     level = lax.broadcasted_iota(jnp.int32, (rates_ref.shape[1], LANES), 0)
     hits = jnp.zeros((rates_ref.shape[1], LANES), F32)
     for m in range(modes_ref.shape[0]):
         hits = hits + jnp.where(level == modes_ref[m : m + 1, :], 1.0, 0.0)
     rates = jnp.broadcast_to(rates_ref[...], (8, rates_ref.shape[1]))
     decay_ref[...] = h * dot(rates, hits, precision=HIGHEST)
-    sub = lax.broadcasted_iota(jnp.int32, (LANES, LANES), 0)
-    for l in range(LINKS):
-        hot = jnp.where(sub == src_ref[l : l + 1, :], 1.0, 0.0).astype(BF16)
-        own_ref[l, 0:LANES, :] = hot
-        own_ref[l, LANES : 2 * LANES, :] = hot
     wide = SLOT * LANES
     i = lax.broadcasted_iota(jnp.int32, (wide, wide), 0)
     p = lax.broadcasted_iota(jnp.int32, (wide, wide), 1)
@@ -197,7 +190,30 @@
                     store(u, kind * 2 * N + c * N + t * 8, kept[u][c][t])
 
 
-def local_part(v_ref, high_ref, low_ref, decay_ref, own_ref, site_ref, base, line, both_ref, even, odd):
+def local_part(
+    v_ref, first_ref, second_ref, decay_ref, src_ref, site_ref, base, line,
+    both_ref, high_ref, low_ref, full,
+):
+    at = lax.broadcasted_iota(jnp.int32, (N, SQ), 1)
+    row = lax.broadcasted_iota(jnp.int32, (N, SQ), 0)
+    group = div24(at)
+    same_second = row == at - group * N
+    by_second = second_ref[...]
+
+    def turns(i, carry):
+        parts = []
+        for j in range(2):
+            a = 2 * i + j
+            block = jnp.where(same_second, jnp.broadcast_to(first_ref[pl.ds(a, 1), :], (N, SQ)), 0.0)
+            parts.append(block - jnp.where(group == a, by_second, 0.0))
+        high, low = split(jnp.concatenate(parts, axis=0))
+        rows = pl.ds(pl.multiple_of(i * 2 * N, 2 * N), 2 * N)
+        high_ref[rows, :] = high
+        low_ref[rows, :] = low
+        return carry
+
+    lax.fori_loop(0, N // 2, turns, 0)
+    sub = lax.broadcasted_iota(jnp.int32, (LANES, LANES), 0)
     real, imag = v_ref[0:SQ, :], v_ref[SQ:ROWS, :]
     real_high, real_low = split(real)
     imag_high, imag_low = split(imag)
@@ -206,7 +222,8 @@
     both_ref[...] = jnp.concatenate([high, low], axis=1)
 
     def fetch(l, place):
-        place[...] = dot(both_ref[...], own_ref[l])
+        hot = jnp.where(sub == src_ref[pl.ds(l, 1), :], 1.0, 0.0).astype(BF16)
+        place[...] = dot(both_ref[...], jnp.concatenate([hot, hot], axis=0))
 
     def pick(l, place):
         site = jnp.broadcast_to(site_ref[pl.ds(l, 1), :], (8, LANES))
@@ -221,15 +238,12 @@
             store,
         )
 
-    def pair(i, carry):
-        fetch(2 * i + 1, odd)
-        pick(2 * i, even)
-        fetch(jnp.minimum(2 * i + 2, LINKS - 1), even)
-        pick(2 * i + 1, odd)
+    def link(l, carry):
+        fetch(l, full)
+        pick(l, full)
         return carry
 
-    fetch(0, even)
-    lax.fori_loop(0, LINKS // 2, pair, 0)
+    lax.fori_loop(0, LINKS, link, 0)
     x_high = jnp.concatenate([real_high, imag_high], axis=1)
     x_low = jnp.concatenate([real_low, imag_low], axis=1)
     turned = dot(high_ref[...], x_high) + dot(high_ref[...], x_low) + dot(low_ref[...], x_high)
@@ -277,18 +291,29 @@
     )
 
 
-def gather_part(got_ref, place_ref, site_ref, coef_ref, base_ref, line_ref, emit, feats, cols):
+def gather_part(
+    got_ref, place_ref, piece_ref, site_ref, coef_ref, base_ref, line_ref, emit, feats, cols
+):
     for k in range(BLOCKS):
         feats[k * LANES : (k + 1) * LANES, :] = got_ref[pl.ds(k, LANES, stride=BLOCKS), :].T
-    wide = jnp.concatenate([feats[p * LINE : (p + 1) * LINE, :] for p in range(PIECES)], axis=1)
-    high, low = split(wide)
-    both = dot(jnp.concatenate([high, low], axis=0), place_ref[...])
-    found = both[0:LINE, :] + both[LINE:, :]
+    high, low = split(feats[...])
+    wide = jnp.concatenate([high, low], axis=1)
+    found = []
+    for pair in range(LINKS // 2):
+        both = dot(wide, place_ref[:, pair * 2 * LANES : (pair + 1) * 2 * LANES])
+        for half in range(2):
+            l = pair * 2 + half
+            piece = jnp.broadcast_to(piece_ref[l : l + 1, :], (LINE, LANES))
+            value = line_ref[l]
+            for p in range(PIECES):
+                part = both[p * LINE : (p + 1) * LINE, half * LANES : (half + 1) * LANES]
+                value = jnp.where(piece == p, part, value)
+            found.append(value)
     sites = [jnp.broadcast_to(site_ref[l : l + 1, :], (8, LANES)) for l in range(LINKS)]
 
     def term(kind, c, l):
         rows = slice(kind * 2 * N, (kind + 1) * 2 * N)
-        x = found[rows, l * LANES : (l + 1) * LANES] + line_ref[l, rows, :]
+        x = found[l][rows]
         re, im = x[0:N], x[N:]
         row = 2 * kind * LINKS + l
         cr = jnp.broadcast_to(coef_ref[row : row + 1, :], (N, LANES))
@@ -317,60 +342,84 @@
                         emit(at, total)
 
 
-SCRATCH = [
-    ((ROWS, LANES), F32),
-    ((LINKS, LINE, LANES), F32),
-    ((ROWS, 2 * LANES), BF16),
-    ((SLOT, ROWS, LANES), F32),
-    ((FEATURES, LANES), F32),
-    ((ROWS, LANES), F32),
-]
-
-
-def advance(weight, got, v, total, tables, site, want):
-    def body(got_ref, v_ref, total_ref, place_ref, high_ref, low_ref, decay_ref, own_ref, pick_ref,
-             coef_ref, site_ref, want_ref, next_ref, send_ref, sum_ref, base, line, both, full, feats, cols):
-        local_part(v_ref, high_ref, low_ref, decay_ref, own_ref, site_ref, base, line, both, full.at[0], full.at[1])
-
+def local(n, v, total, turn, decay, src, site, last=()):
+    add = n > 0
+
+    def body(v_ref, total_ref, first_ref, second_ref, decay_ref, src_ref, site_ref, *refs):
+        refs, (both, high, low, full) = refs[:-4], refs[-4:]
+        base, line = refs[len(last) : len(last) + 2]
+        if add:
+            new = total_ref[...] + NEW[n] * v_ref[...]
+            refs[len(last) + 2][...] = new
+        if last:
+            state_ref, before_ref = refs[:2]
+            refs[-1][...] = ERR[POWERS] / (
+                ABS_TOL + REL_TOL * jnp.maximum(jnp.abs(state_ref[...]), jnp.abs(new))
+            )
+            error = ERR[POWERS - 2] * before_ref[...] + ERR[POWERS - 1] * v_ref[...]
+            both_error = error * (1.0 / ERR[POWERS])
+        local_part(
+            v_ref, first_ref, second_ref, decay_ref, src_ref, site_ref, base, line,
+            both, high, low, full,
+        )
+        if last:
+            base[...] = base[...] + both_error
+
+    return call(
+        body,
+        [((ROWS, LANES), F32), ((LINKS, LINE, LANES), F32)]
+        + [((ROWS, LANES), F32)] * (add + bool(last)),
+        [
+            ((ROWS, 2 * LANES), BF16),
+            ((SQ, SQ), BF16),
+            ((SQ, SQ), BF16),
+            ((ROWS, LANES), F32),
+        ],
+        flops=10**9, name="local", args=(v, total, *turn, decay, src, site, *last),
+        aliases={1: 2} if 1 < n < POWERS - 1 else {},
+    )
+
+
+def advance(got, base, line, place, piece, pick, coef, site, want):
+    def body(got_ref, base_ref, line_ref, place_ref, piece_ref, pick_ref, coef_ref,
+             site_ref, want_ref, next_ref, send_ref, full, feats, cols):
         def emit(at, value):
             next_ref[at : at + 8, :] = value
-            sum_ref[at : at + 8, :] = total_ref[at : at + 8, :] + weight * value
-
-        gather_part(got_ref, place_ref, site_ref, coef_ref, base, line, emit, feats, cols)
+
+        gather_part(
+            got_ref, place_ref, piece_ref, site_ref, coef_ref, base_ref, line_ref, emit, feats, cols
+        )
         pack_part(next_ref, pick_ref, want_ref[...], send_ref, full, feats)
 
     return call(
         body,
-        [((ROWS, LANES), F32), ((BLOCKS * LANES, LANES), F32), ((ROWS, LANES), F32)],
-        SCRATCH, name="advance", args=(got, v, total, *tables, site, want),
-    )
-
-
-def finish(got, v, before, state, new, tables, site):
-    def body(got_ref, v_ref, before_ref, state_ref, new_ref, place_ref, high_ref, low_ref, decay_ref,
-             own_ref, pick_ref, coef_ref, site_ref, out_ref, base, line, both, full, feats, cols, sums):
-        local_part(v_ref, high_ref, low_ref, decay_ref, own_ref, site_ref, base, line, both, full.at[0], full.at[1])
+        [((ROWS, LANES), F32), ((BLOCKS * LANES, LANES), F32)],
+        [((SLOT, ROWS, LANES), F32), ((FEATURES, LANES), F32), ((ROWS, LANES), F32)],
+        name="advance", aliases={1: 0},
+        args=(got, base, line, place, piece, pick, coef, site, want),
+    )
+
+
+def finish(got, base, line, inverse, place, piece, coef, site):
+    def body(got_ref, base_ref, line_ref, inverse_ref, place_ref, piece_ref, coef_ref,
+             site_ref, out_ref, feats, cols, sums):
         sums[...] = jnp.zeros((8, LANES), F32)
 
         def emit(at, value):
             rows = slice(at, at + 8)
-            error = (
-                ERR[POWERS - 2] * before_ref[rows, :]
-                + ERR[POWERS - 1] * v_ref[rows, :]
-                + ERR[POWERS] * value
-            )
-            largest = jnp.maximum(jnp.abs(state_ref[rows, :]), jnp.abs(new_ref[rows, :]))
-            scaled = error / (ABS_TOL + REL_TOL * largest)
+            scaled = value * inverse_ref[rows, :]
             sums[...] = sums[...] + scaled * scaled
 
-        gather_part(got_ref, place_ref, site_ref, coef_ref, base, line, emit, feats, cols)
+        gather_part(
+            got_ref, place_ref, piece_ref, site_ref, coef_ref, base_ref, line_ref, emit, feats, cols
+        )
         out_ref[...] = jnp.broadcast_to(jnp.sum(sums[...], axis=0, keepdims=True), (LANES, LANES))
 
     (out,) = call(
         body,
         [((LANES, LANES), F32)],
-        SCRATCH + [((8, LANES), F32)],
-        name="finish", args=(got, v, before, state, new, *tables, site),
+        [((FEATURES, LANES), F32), ((ROWS, LANES), F32), ((8, LANES), F32)],
+        name="finish", args=(got, base, line, inverse, place, piece, coef, site),
     )
     return out
 
@@ -386,36 +435,42 @@
     state, hamiltonian, mode_rates, ado_modes, link_src, link_site, link_coef, send_ids, step_units
 ):
     v = state.reshape(ROWS, LANES)
-    place, ask = call(
+    place, piece, ask = call(
         plan_body,
-        [((COUPLINGS, COUPLINGS), BF16), ((LANES, LANES), F32)],
+        [((2 * LANES, COUPLINGS), BF16), ((LINKS, LANES), jnp.int32), ((LANES, LANES), F32)],
         flops=10**8, name="plan", args=(link_src, link_site),
     )
     asked = exchange(ask)
-    high, low, decay, own, pick, coef = call(
+    *turn, decay, pick, coef = call(
         tables_body,
         [
-            ((SQ, SQ), BF16),
-            ((SQ, SQ), BF16),
+            ((N, SQ), F32),
+            ((N, SQ), F32),
             ((8, LANES), F32),
-            ((LINKS, 2 * LANES, LANES), BF16),
             ((2 * LANES, SLOT * LANES), BF16),
             ((4 * LINKS, LANES), F32),
         ],
         flops=10**9, name="tables", smem=(0,),
         args=(
-            step_units.reshape(1), hamiltonian, mode_rates.reshape(1, -1), ado_modes, link_src,
+            step_units.reshape(1), hamiltonian, mode_rates.reshape(1, -1), ado_modes,
             link_coef.reshape(4 * LINKS, LANES), send_ids,
         ),
     )
     send, want = first_pack(v, pick, asked)
-    total, before = v, v
-    tables = (place, high, low, decay, own, pick, coef)
-    for n in range(1, POWERS):
+    total = v
+    for n in range(POWERS - 1):
+        got = exchange(send)
+        base, line, *added = local(n, v, total, turn, decay, link_src, link_site)
+        if added:
+            (total,) = added
         before = v
-        v, send, total = advance(NEW[n], exchange(send), before, total, tables, link_site, want)
-    start = state.reshape(ROWS, LANES)
-    sums = exchange(finish(exchange(send), v, before, start, total, tables, link_site))
+        v, send = advance(got, base, line, place, piece, pick, coef, link_site, want)
+    got = exchange(send)
+    start = lax.optimization_barrier((state, v))[0].reshape(ROWS, LANES)
+    base, line, total, inverse = local(
+        POWERS - 1, v, total, turn, decay, link_src, link_site, (start, before)
+    )
+    sums = exchange(finish(got, base, line, inverse, place, piece, coef, link_site))
     entries = state.size * lax.axis_size(ALL)
     return total.reshape(state.shape), jnp.sqrt(jnp.sum(sums) / entries)
 

time: 201 us -> 182 us (0.905)
  blocking collectives: 131 us -> 14.5 us
  waiting for transfers between devices: 2.6 us -> 46.4 us
  starting transfers between devices: 11.7 us -> 46.7 us
  Pallas kernels: 41.1 us -> 53.5 us
  local copies, waits for them, and re-layouts: 8.57 us -> 14.9 us
    all_to_all x8 -> x1, blocking collectives: 131 us -> 14.5 us  [exchange(): moved = lax.all_to_all(flat, ALL, split_axis=0, concat_axis=0, tiled=True)]
    all_to_all x1 -> x8, waiting for transfers between devices: 2.6 us -> 46.4 us  [exchange(): moved = lax.all_to_all(flat, ALL, split_axis=0, concat_axis=0, tiled=True)]
    all_to_all x1 -> x8, starting transfers between devices: 11.7 us -> 46.7 us  [exchange(): moved = lax.all_to_all(flat, ALL, split_axis=0, concat_axis=0, tiled=True)]
    pallas_call x10 -> x17, Pallas kernels: 41.1 us -> 53.5 us  [call(): pl.pallas_call(body, out_shape=[jax.ShapeDtypeStruct(s, d) for s, d in ou...]
    unnamed x26 -> x54, local copies, waits for them, and re-layouts: 8.57 us -> 14.9 us
  transfers between devices with their start and end apart: 1 -> 8, of which waited for: 1 -> 8; matrix products, arithmetic and copies ran while one was open for 0% -> 0% of each run, Pallas kernels for 0% -> 17%
where the time goes in v2:
time: 182 us; the launch traced here: 180 us
  Pallas kernels  53.5 us (29%)
  starting transfers between devices  46.7 us (26%)
  waiting for transfers between devices  46.4 us (25%)
  local copies, waits for them, and re-layouts  14.9 us (8%)
  blocking collectives  14.5 us (8%)
  between operations  3.44 us (2%)
    pallas_call x17, Pallas kernels, call(): pl.pallas_call(body, out_shape=[jax.ShapeDtypeStruct(s, d) for s, d in ou...  53.5 us
    all_to_all x8, starting transfers between devices, exchange(): moved = lax.all_to_all(flat, ALL, split_axis=0, concat_axis=0, tiled=True)  46.7 us
    all_to_all x8, waiting for transfers between devices, exchange(): moved = lax.all_to_all(flat, ALL, split_axis=0, concat_axis=0, tiled=True)  46.4 us
    unnamed x54, local copies, waits for them, and re-layouts  14.9 us
    all_to_all x1, blocking collectives, exchange(): moved = lax.all_to_all(flat, ALL, split_axis=0, concat_axis=0, tiled=True)  14.5 us
  transfers between devices with their start and end apart: 8, of which 8 were waited for; matrix products, arithmetic and copies ran while one was open for 0% of the time, Pallas kernels for 17%

profile of v2, /device:TPU:0, one launch (start us, length us, event | category | flops | bytes accessed | tf_op | source)
XLA Modules:
  0.0 180.1 jit_solution(7647679890819527901)
XLA Ops:
  3.3 11.2 %all-to-all-start = ((f32[128,1,128]{2,1,0:T(1,128)}), f32[128,1,128]{2,1,0:T(1,128)S(1)}, u32[]{:S(2)}, u32[]{:S(2)}) async-start(f32[128,1,128]{2,1,0:T(1,128)} %bitcast.5), calls=%async_computation | async-start | bytes 131072 | tf_op jit(solution)/shard_map/all_to_all | solution.py:430
  16.3 7.2 %all-to-all-done = f32[128,1,128]{2,1,0:T(1,128)S(1)} async-done(((f32[128,1,128]{2,1,0:T(1,128)}), f32[128,1,128]{2,1,0:T(1,128)S(1)}, u32[]{:S(2)}, u32[]{:S(2)}) %all-to-all-start) | async-done | bytes 65568 | tf_op jit(solution)/shard_map/all_to_all | solution.py:430
  23.5 1.6 pack_first.1
  25.1 4.9 %all-to-all-start.1 = ((f32[128,1,768]{2,1,0:T(1,128)}), f32[128,1,768]{2,1,0:T(1,128)S(1)}, u32[]{:S(2)}, u32[]{:S(2)}) async-start(f32[128,1,768]{2,1,0:T(1,128)} %bitcast.7), calls=%async_computation.1 | async-start | bytes 786432 | tf_op jit(solution)/shard_map/all_to_all | solution.py:430
  30.7 4.2 %local.7 = (f32[1152,128]{1,0:T(8,128)S(1)}, f32[8,96,128]{2,1,0:T(8,128)S(1)}) custom-call(f32[1152,128]{1,0:T(8,128)S(1)} %bitcast.36, f32[1152,128]{1,0:T(8,128)S(1)} %bitcast.37, f32[24,576]{1,0:T(8,128)S(1)} %get-tuple-element.49.first_ref, f32[24,576]{1,0:T(8,128)S(1)} %get-tuple-element.50.second_ref, f32[8,128]{1,0:T(8,128)S(1)} %get-tuple-element.51.decay_ref, ...), custom_call_target="tpu_custom_call" | custom-call | flops 1000000000 | bytes 4000000 | tf_op jit(solution)/shard_map/local/pallas_call | solution.py:84
  34.9 6.8 %all-to-all-done.1 = f32[128,1,768]{2,1,0:T(1,128)S(1)} async-done(((f32[128,1,768]{2,1,0:T(1,128)}), f32[128,1,768]{2,1,0:T(1,128)S(1)}, u32[]{:S(2)}, u32[]{:S(2)}) %all-to-all-start.1) | async-done | bytes 393248 | tf_op jit(solution)/shard_map/all_to_all | solution.py:430
  41.6 3.1 %advance.6 = (f32[1152,128]{1,0:T(8,128)S(1)}, f32[768,128]{1,0:T(8,128)}) custom-call(f32[768,128]{1,0:T(8,128)S(1)} %bitcast.33, f32[1152,128]{1,0:T(8,128)S(1)} %get-tuple-element.52.base_ref, f32[8,96,128]{2,1,0:T(8,128)S(1)} %get-tuple-element.53.line_ref, bf16[256,1024]{1,0:T(8,128)(2,1)S(1)} %get-tuple-element.54.place_ref, ...), custom_call_target="tpu_custom_call", output_to_operand_aliasing={{0}: (1, {})} | custom-call | flops 1000000 | bytes 4000000 | tf_op jit(solution)/shard_map/advance/pallas_call | solution.py:84
  44.7 5.1 %all-to-all-start.2 = ((f32[128,1,768]{2,1,0:T(1,128)}), f32[128,1,768]{2,1,0:T(1,128)S(1)}, u32[]{:S(2)}, u32[]{:S(2)}) async-start(f32[128,1,768]{2,1,0:T(1,128)} %bitcast.9), calls=%async_computation.2 | async-start | bytes 786432 | tf_op jit(solution)/shard_map/all_to_all | solution.py:430
  49.8 4.2 %local.8 = (f32[1152,128]{1,0:T(8,128)S(1)}, f32[8,96,128]{2,1,0:T(8,128)S(1)}, f32[1152,128]{1,0:T(8,128)S(1)}) custom-call(f32[1152,128]{1,0:T(8,128)S(1)} %get-tuple-element.59.v_ref, f32[1152,128]{1,0:T(8,128)S(1)} %bitcast.38, f32[24,576]{1,0:T(8,128)S(1)} %get-tuple-element.49.first_ref, f32[24,576]{1,0:T(8,128)S(1)} %get-tuple-element.50.second_ref, ...), custom_call_target="tpu_custom_call" | custom-call | flops 1000000000 | bytes 4000000 | tf_op jit(solution)/shard_map/local/pallas_call | solution.py:84
  54.8 6.6 %all-to-all-done.2 = f32[128,1,768]{2,1,0:T(1,128)S(1)} async-done(((f32[128,1,768]{2,1,0:T(1,128)}), f32[128,1,768]{2,1,0:T(1,128)S(1)}, u32[]{:S(2)}, u32[]{:S(2)}) %all-to-all-start.2) | async-done | bytes 393248 | tf_op jit(solution)/shard_map/all_to_all | solution.py:430
  61.4 3.1 %advance.7 = (f32[1152,128]{1,0:T(8,128)S(1)}, f32[768,128]{1,0:T(8,128)}) custom-call(f32[768,128]{1,0:T(8,128)S(1)} %bitcast.34, f32[1152,128]{1,0:T(8,128)S(1)} %get-tuple-element.60.base_ref, f32[8,96,128]{2,1,0:T(8,128)S(1)} %get-tuple-element.61.line_ref, bf16[256,1024]{1,0:T(8,128)(2,1)S(1)} %get-tuple-element.54.place_ref, ...), custom_call_target="tpu_custom_call", output_to_operand_aliasing={{0}: (1, {})} | custom-call | flops 1000000 | bytes 4000000 | tf_op jit(solution)/shard_map/advance/pallas_call | solution.py:84
  64.5 5.3 %all-to-all-start.3 = ((f32[128,1,768]{2,1,0:T(1,128)}), f32[128,1,768]{2,1,0:T(1,128)S(1)}, u32[]{:S(2)}, u32[]{:S(2)}) async-start(f32[128,1,768]{2,1,0:T(1,128)} %bitcast.11), calls=%async_computation.3 | async-start | bytes 786432 | tf_op jit(solution)/shard_map/all_to_all | solution.py:430
  70.8 4.3 %local.9 = (f32[1152,128]{1,0:T(8,128)S(1)}, f32[8,96,128]{2,1,0:T(8,128)S(1)}, f32[1152,128]{1,0:T(8,128)S(1)}) custom-call(f32[1152,128]{1,0:T(8,128)S(1)} %get-tuple-element.63.v_ref, f32[1152,128]{1,0:T(8,128)S(1)} %copy-done.15, f32[24,576]{1,0:T(8,128)S(1)} %get-tuple-element.49.first_ref, ...), custom_call_target="tpu_custom_call", output_to_operand_aliasing={{2}: (1, {})} | custom-call | flops 1000000000 | bytes 4000000 | tf_op jit(solution)/shard_map/local/pallas_call | solution.py:84
  75.9 5.3 %all-to-all-done.3 = f32[128,1,768]{2,1,0:T(1,128)S(1)} async-done(((f32[128,1,768]{2,1,0:T(1,128)}), f32[128,1,768]{2,1,0:T(1,128)S(1)}, u32[]{:S(2)}, u32[]{:S(2)}) %all-to-all-start.3) | async-done | bytes 393248 | tf_op jit(solution)/shard_map/all_to_all | solution.py:430
  81.2 3.1 %advance.8 = (f32[1152,128]{1,0:T(8,128)S(1)}, f32[768,128]{1,0:T(8,128)}) custom-call(f32[768,128]{1,0:T(8,128)S(1)} %bitcast.30, f32[1152,128]{1,0:T(8,128)S(1)} %get-tuple-element.65.base_ref, f32[8,96,128]{2,1,0:T(8,128)S(1)} %get-tuple-element.66.line_ref, bf16[256,1024]{1,0:T(8,128)(2,1)S(1)} %get-tuple-element.54.place_ref, ...), custom_call_target="tpu_custom_call", output_to_operand_aliasing={{0}: (1, {})} | custom-call | flops 1000000 | bytes 4000000 | tf_op jit(solution)/shard_map/advance/pallas_call | solution.py:84
  84.3 5.1 %all-to-all-start.4 = ((f32[128,1,768]{2,1,0:T(1,128)}), f32[128,1,768]{2,1,0:T(1,128)S(1)}, u32[]{:S(2)}, u32[]{:S(2)}) async-start(f32[128,1,768]{2,1,0:T(1,128)} %bitcast.13), calls=%async_computation.4 | async-start | bytes 786432 | tf_op jit(solution)/shard_map/all_to_all | solution.py:430
  90.4 4.3 %local.10 = (f32[1152,128]{1,0:T(8,128)S(1)}, f32[8,96,128]{2,1,0:T(8,128)S(1)}, f32[1152,128]{1,0:T(8,128)S(1)}) custom-call(f32[1152,128]{1,0:T(8,128)S(1)} %get-tuple-element.68.v_ref, f32[1152,128]{1,0:T(8,128)S(1)} %copy-done.17, f32[24,576]{1,0:T(8,128)S(1)} %get-tuple-element.49.first_ref, ...), custom_call_target="tpu_custom_call", output_to_operand_aliasing={{2}: (1, {})} | custom-call | flops 1000000000 | bytes 4000000 | tf_op jit(solution)/shard_map/local/pallas_call | solution.py:84
  95.6 5.4 %all-to-all-done.4 = f32[128,1,768]{2,1,0:T(1,128)S(1)} async-done(((f32[128,1,768]{2,1,0:T(1,128)}), f32[128,1,768]{2,1,0:T(1,128)S(1)}, u32[]{:S(2)}, u32[]{:S(2)}) %all-to-all-start.4) | async-done | bytes 393248 | tf_op jit(solution)/shard_map/all_to_all | solution.py:430
  101.0 3.1 %advance.9 = (f32[1152,128]{1,0:T(8,128)S(1)}, f32[768,128]{1,0:T(8,128)}) custom-call(f32[768,128]{1,0:T(8,128)S(1)} %bitcast.31, f32[1152,128]{1,0:T(8,128)S(1)} %get-tuple-element.70.base_ref, f32[8,96,128]{2,1,0:T(8,128)S(1)} %get-tuple-element.71.line_ref, bf16[256,1024]{1,0:T(8,128)(2,1)S(1)} %get-tuple-element.54.place_ref, ...), custom_call_target="tpu_custom_call", output_to_operand_aliasing={{0}: (1, {})} | custom-call | flops 1000000 | bytes 4000000 | tf_op jit(solution)/shard_map/advance/pallas_call | solution.py:84
  104.1 5.1 %all-to-all-start.5 = ((f32[128,1,768]{2,1,0:T(1,128)}), f32[128,1,768]{2,1,0:T(1,128)S(1)}, u32[]{:S(2)}, u32[]{:S(2)}) async-start(f32[128,1,768]{2,1,0:T(1,128)} %bitcast.15), calls=%async_computation.5 | async-start | bytes 786432 | tf_op jit(solution)/shard_map/all_to_all | solution.py:430
  110.2 4.3 %local.11 = (f32[1152,128]{1,0:T(8,128)S(1)}, f32[8,96,128]{2,1,0:T(8,128)S(1)}, f32[1152,128]{1,0:T(8,128)S(1)}) custom-call(f32[1152,128]{1,0:T(8,128)S(1)} %get-tuple-element.73.v_ref, f32[1152,128]{1,0:T(8,128)S(1)} %copy-done.19, f32[24,576]{1,0:T(8,128)S(1)} %get-tuple-element.49.first_ref, ...), custom_call_target="tpu_custom_call", output_to_operand_aliasing={{2}: (1, {})} | custom-call | flops 1000000000 | bytes 4000000 | tf_op jit(solution)/shard_map/local/pallas_call | solution.py:84
  115.4 5.4 %all-to-all-done.5 = f32[128,1,768]{2,1,0:T(1,128)S(1)} async-done(((f32[128,1,768]{2,1,0:T(1,128)}), f32[128,1,768]{2,1,0:T(1,128)S(1)}, u32[]{:S(2)}, u32[]{:S(2)}) %all-to-all-start.5) | async-done | bytes 393248 | tf_op jit(solution)/shard_map/all_to_all | solution.py:430
  120.8 3.1 %advance.10 = (f32[1152,128]{1,0:T(8,128)S(1)}, f32[768,128]{1,0:T(8,128)}) custom-call(f32[768,128]{1,0:T(8,128)S(1)} %bitcast.32, f32[1152,128]{1,0:T(8,128)S(1)} %get-tuple-element.75.base_ref, f32[8,96,128]{2,1,0:T(8,128)S(1)} %get-tuple-element.76.line_ref, bf16[256,1024]{1,0:T(8,128)(2,1)S(1)} %get-tuple-element.54.place_ref, ...), custom_call_target="tpu_custom_call", output_to_operand_aliasing={{0}: (1, {})} | custom-call | flops 1000000 | bytes 4000000 | tf_op jit(solution)/shard_map/advance/pallas_call | solution.py:84
  123.9 5.1 %all-to-all-start.6 = ((f32[128,1,768]{2,1,0:T(1,128)}), f32[128,1,768]{2,1,0:T(1,128)S(1)}, u32[]{:S(2)}, u32[]{:S(2)}) async-start(f32[128,1,768]{2,1,0:T(1,128)} %bitcast.17), calls=%async_computation.6 | async-start | bytes 786432 | tf_op jit(solution)/shard_map/all_to_all | solution.py:430
  130.0 4.3 %local.12 = (f32[1152,128]{1,0:T(8,128)S(1)}, f32[8,96,128]{2,1,0:T(8,128)S(1)}, f32[1152,128]{1,0:T(8,128)S(1)}) custom-call(f32[1152,128]{1,0:T(8,128)S(1)} %get-tuple-element.78.v_ref.refs_1_, f32[1152,128]{1,0:T(8,128)S(1)} %copy-done.21, f32[24,576]{1,0:T(8,128)S(1)} %get-tuple-element.49.first_ref, ...), custom_call_target="tpu_custom_call", output_to_operand_aliasing={{2}: (1, {})} | custom-call | flops 1000000000 | bytes 4000000 | tf_op jit(solution)/shard_map/local/pallas_call | solution.py:84
  135.1 5.4 %all-to-all-done.6 = f32[128,1,768]{2,1,0:T(1,128)S(1)} async-done(((f32[128,1,768]{2,1,0:T(1,128)}), f32[128,1,768]{2,1,0:T(1,128)S(1)}, u32[]{:S(2)}, u32[]{:S(2)}) %all-to-all-start.6) | async-done | bytes 393248 | tf_op jit(solution)/shard_map/all_to_all | solution.py:430
  140.6 3.1 %advance.11 = (f32[1152,128]{1,0:T(8,128)S(1)}, f32[768,128]{1,0:T(8,128)}) custom-call(f32[768,128]{1,0:T(8,128)S(1)} %bitcast.29, f32[1152,128]{1,0:T(8,128)S(1)} %get-tuple-element.80.base_ref, f32[8,96,128]{2,1,0:T(8,128)S(1)} %get-tuple-element.81.line_ref, bf16[256,1024]{1,0:T(8,128)(2,1)S(1)} %get-tuple-element.54.place_ref, ...), custom_call_target="tpu_custom_call", output_to_operand_aliasing={{0}: (1, {})} | custom-call | flops 1000000 | bytes 4000000 | tf_op jit(solution)/shard_map/advance/pallas_call | solution.py:84
  143.6 5.1 %all-to-all-start.7 = ((f32[128,1,768]{2,1,0:T(1,128)}), f32[128,1,768]{2,1,0:T(1,128)S(1)}, u32[]{:S(2)}, u32[]{:S(2)}) async-start(f32[128,1,768]{2,1,0:T(1,128)} %bitcast.21), calls=%async_computation.7 | async-start | bytes 786432 | tf_op jit(solution)/shard_map/all_to_all | solution.py:430
  150.8 4.4 %local.13 = (f32[1152,128]{1,0:T(8,128)S(1)}, f32[8,96,128]{2,1,0:T(8,128)S(1)}, f32[1152,128]{1,0:T(8,128)}, f32[1152,128]{1,0:T(8,128)S(1)}) custom-call(f32[1152,128]{1,0:T(8,128)S(1)} %get-tuple-element.82.v_ref, f32[1152,128]{1,0:T(8,128)S(1)} %copy-done.23, f32[24,576]{1,0:T(8,128)S(1)} %get-tuple-element.49.first_ref, f32[24,576]{1,0:T(8,128)S(1)} %copy-done.26, ...), custom_call_target="tpu_custom_call" | custom-call | flops 1000000000 | bytes 4000000 | tf_op jit(solution)/shard_map/local/pallas_call | solution.py:84
  156.1 4.3 %all-to-all-done.7 = f32[128,1,768]{2,1,0:T(1,128)S(1)} async-done(((f32[128,1,768]{2,1,0:T(1,128)}), f32[128,1,768]{2,1,0:T(1,128)S(1)}, u32[]{:S(2)}, u32[]{:S(2)}) %all-to-all-start.7) | async-done | bytes 393248 | tf_op jit(solution)/shard_map/all_to_all | solution.py:430
  161.3 1.7 finish.1
  163.0 14.5 %all_to_all.45 = f32[128,1,128]{2,1,0:T(1,128)S(1)} all-to-all(f32[128,1,128]{2,1,0:T(1,128)S(1)} %bitcast.41), channel_id=1, replica_groups=mesh['grp'=2,'dev'=64] {'grp','dev'}, dimensions={0} | all-to-all | bytes 131072 | tf_op jit(solution)/shard_map/all_to_all | solution.py:430
  (57 shorter events, 17.4 us)
Async XLA Ops:
  0.6 0.7 copy-start.5
  1.3 0.7 copy-start.9
  3.2 11.9 %copy-start.7 = (f32[4,8,128]{2,1,0:T(8,128)S(1)}, f32[4,8,128]{2,1,0:T(8,128)}, u32[]{:S(2)}) copy-start(f32[4,8,128]{2,1,0:T(8,128)} %param.15) | copy-start | bytes 49156
  3.2 11.9 %copy-start.8 = (f32[24,24]{1,0:T(8,128)S(1)}, f32[24,24]{1,0:T(8,128)}, u32[]{:S(2)}) copy-start(f32[24,24]{1,0:T(8,128)} %ham_ref.1) | copy-start | bytes 6916
  3.3 20.3 %all-to-all-start = ((f32[128,1,128]{2,1,0:T(1,128)}), f32[128,1,128]{2,1,0:T(1,128)S(1)}, u32[]{:S(2)}, u32[]{:S(2)}) async-start(f32[128,1,128]{2,1,0:T(1,128)} %bitcast.5), calls=%async_computation | async-start | bytes 131072 | tf_op jit(solution)/shard_map/all_to_all | solution.py:430
  15.8 7.7 %copy-start = (f32[2,24,24,128]{3,2,1,0:T(8,128)S(1)}, f32[2,24,24,128]{3,2,1,0:T(8,128)}, u32[]{:S(2)}) copy-start(f32[2,24,24,128]{3,2,1,0:T(8,128)} %param.9) | copy-start | bytes 1769476
  16.3 92.9 %copy-start.24 = (f32[24,576]{1,0:T(8,128)}, f32[24,576]{1,0:T(8,128)S(1)}, u32[]{:S(2)}) copy-start(f32[24,576]{1,0:T(8,128)S(1)} %get-tuple-element.50.second_ref) | copy-start | bytes 165892
  25.1 4.9 %copy-start.10 = (s32[8,128]{1,0:T(8,128)S(1)}, s32[8,128]{1,0:T(8,128)}, u32[]{:S(2)}) copy-start(s32[8,128]{1,0:T(8,128)} %src_ref.15) | copy-start | bytes 12292
  25.1 16.5 %all-to-all-start.1 = ((f32[128,1,768]{2,1,0:T(1,128)}), f32[128,1,768]{2,1,0:T(1,128)S(1)}, u32[]{:S(2)}, u32[]{:S(2)}) async-start(f32[128,1,768]{2,1,0:T(1,128)} %bitcast.7), calls=%async_computation.1 | async-start | bytes 786432 | tf_op jit(solution)/shard_map/all_to_all | solution.py:430
  30.0 0.7 copy-start.6
  44.7 16.7 %all-to-all-start.2 = ((f32[128,1,768]{2,1,0:T(1,128)}), f32[128,1,768]{2,1,0:T(1,128)S(1)}, u32[]{:S(2)}, u32[]{:S(2)}) async-start(f32[128,1,768]{2,1,0:T(1,128)} %bitcast.9), calls=%async_computation.2 | async-start | bytes 786432 | tf_op jit(solution)/shard_map/all_to_all | solution.py:430
  54.0 0.8 copy-start.14
  64.5 16.7 %all-to-all-start.3 = ((f32[128,1,768]{2,1,0:T(1,128)}), f32[128,1,768]{2,1,0:T(1,128)S(1)}, u32[]{:S(2)}, u32[]{:S(2)}) async-start(f32[128,1,768]{2,1,0:T(1,128)} %bitcast.11), calls=%async_computation.3 | async-start | bytes 786432 | tf_op jit(solution)/shard_map/all_to_all | solution.py:430
  69.8 1.1 copy-start.15
  75.1 0.8 copy-start.16
  84.3 16.7 %all-to-all-start.4 = ((f32[128,1,768]{2,1,0:T(1,128)}), f32[128,1,768]{2,1,0:T(1,128)S(1)}, u32[]{:S(2)}, u32[]{:S(2)}) async-start(f32[128,1,768]{2,1,0:T(1,128)} %bitcast.13), calls=%async_computation.4 | async-start | bytes 786432 | tf_op jit(solution)/shard_map/all_to_all | solution.py:430
  89.4 1.1 copy-start.17
  94.8 0.8 copy-start.18
  104.1 16.7 %all-to-all-start.5 = ((f32[128,1,768]{2,1,0:T(1,128)}), f32[128,1,768]{2,1,0:T(1,128)S(1)}, u32[]{:S(2)}, u32[]{:S(2)}) async-start(f32[128,1,768]{2,1,0:T(1,128)} %bitcast.15), calls=%async_computation.5 | async-start | bytes 786432 | tf_op jit(solution)/shard_map/all_to_all | solution.py:430
  109.2 1.1 copy-start.19
  114.5 0.8 copy-start.20
  123.9 10.5 %copy-start.1 = (f32[1152,128]{1,0:T(8,128)}, f32[1152,128]{1,0:T(8,128)S(1)}, u32[]{:S(2)}) copy-start(f32[1152,128]{1,0:T(8,128)S(1)} %get-tuple-element.78.v_ref.refs_1_) | copy-start | bytes 1769476
  123.9 5.1 %copy-start.25 = (f32[24,576]{1,0:T(8,128)S(1)}, f32[24,576]{1,0:T(8,128)}, u32[]{:S(2)}) copy-start(f32[24,576]{1,0:T(8,128)} %copy-done.24) | copy-start | bytes 165892
  123.9 16.7 %all-to-all-start.6 = ((f32[128,1,768]{2,1,0:T(1,128)}), f32[128,1,768]{2,1,0:T(1,128)S(1)}, u32[]{:S(2)}, u32[]{:S(2)}) async-start(f32[128,1,768]{2,1,0:T(1,128)} %bitcast.17), calls=%async_computation.6 | async-start | bytes 786432 | tf_op jit(solution)/shard_map/all_to_all | solution.py:430
  128.9 1.1 copy-start.21
  134.3 0.8 copy-start.22
  143.6 5.1 %copy-start.26 = (f32[24,576]{1,0:T(8,128)S(1)}, f32[24,576]{1,0:T(8,128)}, u32[]{:S(2)}) copy-start(f32[24,576]{1,0:T(8,128)} %copy-done.24) | copy-start | bytes 165892
  143.6 16.7 %all-to-all-start.7 = ((f32[128,1,768]{2,1,0:T(1,128)}), f32[128,1,768]{2,1,0:T(1,128)S(1)}, u32[]{:S(2)}, u32[]{:S(2)}) async-start(f32[128,1,768]{2,1,0:T(1,128)} %bitcast.21), calls=%async_computation.7 | async-start | bytes 786432 | tf_op jit(solution)/shard_map/all_to_all | solution.py:430
  148.7 1.1 copy-start.2
  149.8 1.1 copy-start.23
  155.3 0.8 copy-start.3
  160.3 1.0 copy-start.4
  (3 other events, 2.0 us)

commit v3 on v2

--- a/solution.py
+++ b/solution.py
@@ -244,12 +244,24 @@
         return carry
 
     lax.fori_loop(0, LINKS, link, 0)
-    x_high = jnp.concatenate([real_high, imag_high], axis=1)
-    x_low = jnp.concatenate([real_low, imag_low], axis=1)
-    turned = dot(high_ref[...], x_high) + dot(high_ref[...], x_low) + dot(low_ref[...], x_high)
-    decay = jnp.broadcast_to(decay_ref[0:1, :], (SQ, LANES))
-    base[0:SQ, :] = turned[:, LANES:] - decay * real
-    base[SQ:ROWS, :] = -turned[:, :LANES] - decay * imag
+    chunk = SQ // 3
+    decay = jnp.broadcast_to(decay_ref[0:1, :], (chunk, LANES))
+
+    def commute(i, carry):
+        rows = pl.ds(pl.multiple_of(i * chunk, chunk), chunk)
+        after = pl.ds(pl.multiple_of(SQ + i * chunk, chunk), chunk)
+        x_high, x_low = (
+            jnp.concatenate([both_ref[0:SQ, half], both_ref[SQ:ROWS, half]], axis=1)
+            for half in (slice(0, LANES), slice(LANES, 2 * LANES))
+        )
+        turned = (
+            dot(high_ref[rows, :], x_high) + dot(high_ref[rows, :], x_low) + dot(low_ref[rows, :], x_high)
+        )
+        base[rows, :] = turned[:, LANES:] - decay * v_ref[rows, :]
+        base[after, :] = -turned[:, :LANES] - decay * v_ref[after, :]
+        return carry
+
+    lax.fori_loop(0, 3, commute, 0)
 
 
 def pack_part(v_ref, pick_ref, sites, send_ref, full, feats):
@@ -303,12 +315,22 @@
         both = dot(wide, place_ref[:, pair * 2 * LANES : (pair + 1) * 2 * LANES])
         for half in range(2):
             l = pair * 2 + half
-            piece = jnp.broadcast_to(piece_ref[l : l + 1, :], (LINE, LANES))
-            value = line_ref[l]
+            piece = jnp.broadcast_to(piece_ref[l : l + 1, :], (8, LANES))
+            if line_ref is None:
+                tiles = [jnp.zeros((8, LANES), F32)] * (LINE // 8)
+            else:
+                tiles = [line_ref[l, f : f + 8, :] for f in range(0, LINE, 8)]
             for p in range(PIECES):
-                part = both[p * LINE : (p + 1) * LINE, half * LANES : (half + 1) * LANES]
-                value = jnp.where(piece == p, part, value)
-            found.append(value)
+                hit = piece == p
+                for t in range(LINE // 8):
+                    f = p * LINE + t * 8
+                    part = both[f : f + 8, half * LANES : (half + 1) * LANES]
+                    tiles[t] = jnp.where(hit, part, tiles[t])
+            found.append(jnp.concatenate(tiles, axis=0))
+    scatter_part(found, site_ref, coef_ref, base_ref, emit, cols)
+
+
+def scatter_part(found, site_ref, coef_ref, base_ref, emit, cols):
     sites = [jnp.broadcast_to(site_ref[l : l + 1, :], (8, LANES)) for l in range(LINKS)]
 
     def term(kind, c, l):
@@ -328,13 +350,14 @@
                 hits = [site == k for site in sites]
                 for t in range(3):
                     if kind:
-                        total = jnp.zeros((8, LANES), F32)
+                        total = None
                     else:
                         at = c * SQ + k * N + t * 8
                         total = base_ref[at : at + 8, :]
                         total = total + cols[pl.ds(c * SQ + t * 8 * N + k, 8, stride=N), :]
                     for l in range(LINKS):
-                        total = total + jnp.where(hits[l], terms[l][t * 8 : t * 8 + 8], 0.0)
+                        part = jnp.where(hits[l], terms[l][t * 8 : t * 8 + 8], 0.0)
+                        total = part if total is None else total + part
                     if kind:
                         at = c * SQ + k * N + t * 8
                         cols[at : at + 8, :] = total
@@ -346,37 +369,44 @@
     add = n > 0
 
     def body(v_ref, total_ref, first_ref, second_ref, decay_ref, src_ref, site_ref, *refs):
-        refs, (both, high, low, full) = refs[:-4], refs[-4:]
-        base, line = refs[len(last) : len(last) + 2]
+        inputs, refs = refs[: len(last)], refs[len(last) :]
+        if last:
+            state_ref, before_ref, coef_ref = inputs
+            base, sum_ref, inverse_ref, both, high, low, full, kept, line, cols = refs
+        elif add:
+            base, line, sum_ref, both, high, low, full = refs
+        else:
+            base, line, both, high, low, full = refs
         if add:
-            new = total_ref[...] + NEW[n] * v_ref[...]
-            refs[len(last) + 2][...] = new
+            sum_ref[...] = total_ref[...] + NEW[n] * v_ref[...]
         if last:
-            state_ref, before_ref = refs[:2]
-            refs[-1][...] = ERR[POWERS] / (
-                ABS_TOL + REL_TOL * jnp.maximum(jnp.abs(state_ref[...]), jnp.abs(new))
+            inverse_ref[...] = ERR[POWERS] / (
+                ABS_TOL + REL_TOL * jnp.maximum(jnp.abs(state_ref[...]), jnp.abs(sum_ref[...]))
             )
             error = ERR[POWERS - 2] * before_ref[...] + ERR[POWERS - 1] * v_ref[...]
-            both_error = error * (1.0 / ERR[POWERS])
+            kept[...] = error * (1.0 / ERR[POWERS])
         local_part(
-            v_ref, first_ref, second_ref, decay_ref, src_ref, site_ref, base, line,
-            both, high, low, full,
+            v_ref, first_ref, second_ref, decay_ref, src_ref, site_ref,
+            full if last else base, line, both, high, low, full,
         )
         if last:
-            base[...] = base[...] + both_error
-
+            kept[...] = kept[...] + full[...]
+
+            def emit(at, value):
+                base[at : at + 8, :] = value
+
+            found = [line[l] for l in range(LINKS)]
+            scatter_part(found, site_ref, coef_ref, kept, emit, cols)
+
+    square = ((ROWS, LANES), F32)
+    lines_of_links = ((LINKS, LINE, LANES), F32)
     return call(
         body,
-        [((ROWS, LANES), F32), ((LINKS, LINE, LANES), F32)]
-        + [((ROWS, LANES), F32)] * (add + bool(last)),
-        [
-            ((ROWS, 2 * LANES), BF16),
-            ((SQ, SQ), BF16),
-            ((SQ, SQ), BF16),
-            ((ROWS, LANES), F32),
-        ],
+        [square] * 3 if last else [square, lines_of_links] + [square] * add,
+        [((ROWS, 2 * LANES), BF16), ((SQ, SQ), BF16), ((SQ, SQ), BF16), square]
+        + ([square, lines_of_links, square] if last else []),
         flops=10**9, name="local", args=(v, total, *turn, decay, src, site, *last),
-        aliases={1: 2} if 1 < n < POWERS - 1 else {},
+        aliases={1: 1} if last else {1: 2} if n > 1 else {},
     )
 
 
@@ -400,8 +430,8 @@
     )
 
 
-def finish(got, base, line, inverse, place, piece, coef, site):
-    def body(got_ref, base_ref, line_ref, inverse_ref, place_ref, piece_ref, coef_ref,
+def finish(got, base, inverse, place, piece, coef, site):
+    def body(got_ref, base_ref, inverse_ref, place_ref, piece_ref, coef_ref,
              site_ref, out_ref, feats, cols, sums):
         sums[...] = jnp.zeros((8, LANES), F32)
 
@@ -411,7 +441,7 @@
             sums[...] = sums[...] + scaled * scaled
 
         gather_part(
-            got_ref, place_ref, piece_ref, site_ref, coef_ref, base_ref, line_ref, emit, feats, cols
+            got_ref, place_ref, piece_ref, site_ref, coef_ref, base_ref, None, emit, feats, cols
         )
         out_ref[...] = jnp.broadcast_to(jnp.sum(sums[...], axis=0, keepdims=True), (LANES, LANES))
 
@@ -419,7 +449,7 @@
         body,
         [((LANES, LANES), F32)],
         [((FEATURES, LANES), F32), ((ROWS, LANES), F32), ((8, LANES), F32)],
-        name="finish", args=(got, base, line, inverse, place, piece, coef, site),
+        name="finish", args=(got, base, inverse, place, piece, coef, site),
     )
     return out
 
@@ -467,10 +497,10 @@
         v, send = advance(got, base, line, place, piece, pick, coef, link_site, want)
     got = exchange(send)
     start = lax.optimization_barrier((state, v))[0].reshape(ROWS, LANES)
-    base, line, total, inverse = local(
-        POWERS - 1, v, total, turn, decay, link_src, link_site, (start, before)
-    )
-    sums = exchange(finish(got, base, line, inverse, place, piece, coef, link_site))
+    base, total, inverse = local(
+        POWERS - 1, v, total, turn, decay, link_src, link_site, (start, before, coef)
+    )
+    sums = exchange(finish(got, base, inverse, place, piece, coef, link_site))
     entries = state.size * lax.axis_size(ALL)
     return total.reshape(state.shape), jnp.sqrt(jnp.sum(sums) / entries)
 

time: 182 us -> 181 us (level)
  local copies, waits for them, and re-layouts: 14.9 us -> 3.78 us
  Pallas kernels: 53.5 us -> 63.3 us
    unnamed x54 -> x30, local copies, waits for them, and re-layouts: 14.9 us -> 3.78 us
    pallas_call x17, Pallas kernels: 53.5 us -> 63.3 us  [call(): pl.pallas_call(body, out_shape=[jax.ShapeDtypeStruct(s, d) for s, d in ou...]
  transfers between devices with their start and end apart: 8 -> 8, of which waited for: 8 -> 8; matrix products, arithmetic and copies ran while one was open for 0% -> 0% of each run, Pallas kernels for 17% -> 22%
where the time goes in v3:
time: 181 us; the launch traced here: 179 us
  Pallas kernels  63.3 us (35%)
  starting transfers between devices  46.9 us (26%)
  waiting for transfers between devices  46.5 us (26%)
  blocking collectives  14.9 us (8%)
  local copies, waits for them, and re-layouts  3.78 us (2%)
  between operations  3.3 us (2%)
    pallas_call x17, Pallas kernels, call(): pl.pallas_call(body, out_shape=[jax.ShapeDtypeStruct(s, d) for s, d in ou...  63.3 us
    all_to_all x8, starting transfers between devices, exchange(): moved = lax.all_to_all(flat, ALL, split_axis=0, concat_axis=0, tiled=True)  46.9 us
    all_to_all x8, waiting for transfers between devices, exchange(): moved = lax.all_to_all(flat, ALL, split_axis=0, concat_axis=0, tiled=True)  46.5 us
    all_to_all x1, blocking collectives, exchange(): moved = lax.all_to_all(flat, ALL, split_axis=0, concat_axis=0, tiled=True)  14.9 us
    unnamed x30, local copies, waits for them, and re-layouts  3.78 us
  transfers between devices with their start and end apart: 8, of which 8 were waited for; matrix products, arithmetic and copies ran while one was open for 0% of the time, Pallas kernels for 22%

profile of v3, /device:TPU:0, one launch (start us, length us, event | category | flops | bytes accessed | tf_op | source)
XLA Modules:
  0.0 179.4 jit_solution(11726530949310714938)
XLA Ops:
  3.3 11.2 %all-to-all-start = ((f32[128,1,128]{2,1,0:T(1,128)}), f32[128,1,128]{2,1,0:T(1,128)S(1)}, u32[]{:S(2)}, u32[]{:S(2)}) async-start(f32[128,1,128]{2,1,0:T(1,128)} %bitcast.5), calls=%async_computation | async-start | bytes 131072 | tf_op jit(solution)/shard_map/all_to_all | solution.py:460
  16.3 7.2 %all-to-all-done = f32[128,1,128]{2,1,0:T(1,128)S(1)} async-done(((f32[128,1,128]{2,1,0:T(1,128)}), f32[128,1,128]{2,1,0:T(1,128)S(1)}, u32[]{:S(2)}, u32[]{:S(2)}) %all-to-all-start) | async-done | bytes 65568 | tf_op jit(solution)/shard_map/all_to_all | solution.py:460
  23.5 1.6 pack_first.1
  25.1 4.9 %all-to-all-start.1 = ((f32[128,1,768]{2,1,0:T(1,128)}), f32[128,1,768]{2,1,0:T(1,128)S(1)}, u32[]{:S(2)}, u32[]{:S(2)}) async-start(f32[128,1,768]{2,1,0:T(1,128)} %bitcast.7), calls=%async_computation.1 | async-start | bytes 786432 | tf_op jit(solution)/shard_map/all_to_all | solution.py:460
  30.7 4.3 %local.7 = (f32[1152,128]{1,0:T(8,128)S(1)}, f32[8,96,128]{2,1,0:T(8,128)S(1)}) custom-call(f32[1152,128]{1,0:T(8,128)S(1)} %bitcast.36, f32[1152,128]{1,0:T(8,128)S(1)} %bitcast.37, f32[24,576]{1,0:T(8,128)S(1)} %get-tuple-element.48.first_ref, f32[24,576]{1,0:T(8,128)S(1)} %get-tuple-element.49.second_ref, f32[8,128]{1,0:T(8,128)S(1)} %get-tuple-element.50.decay_ref, ...), custom_call_target="tpu_custom_call" | custom-call | flops 1000000000 | bytes 4000000 | tf_op jit(solution)/shard_map/local/pallas_call | solution.py:84
  35.0 6.6 %all-to-all-done.1 = f32[128,1,768]{2,1,0:T(1,128)S(1)} async-done(((f32[128,1,768]{2,1,0:T(1,128)}), f32[128,1,768]{2,1,0:T(1,128)S(1)}, u32[]{:S(2)}, u32[]{:S(2)}) %all-to-all-start.1) | async-done | bytes 393248 | tf_op jit(solution)/shard_map/all_to_all | solution.py:460
  41.6 3.1 %advance.6 = (f32[1152,128]{1,0:T(8,128)S(1)}, f32[768,128]{1,0:T(8,128)}) custom-call(f32[768,128]{1,0:T(8,128)S(1)} %bitcast.33, f32[1152,128]{1,0:T(8,128)S(1)} %get-tuple-element.51.base_ref, f32[8,96,128]{2,1,0:T(8,128)S(1)} %get-tuple-element.52.line_ref, bf16[256,1024]{1,0:T(8,128)(2,1)S(1)} %get-tuple-element.53.place_ref, ...), custom_call_target="tpu_custom_call", output_to_operand_aliasing={{0}: (1, {})} | custom-call | flops 1000000 | bytes 4000000 | tf_op jit(solution)/shard_map/advance/pallas_call | solution.py:84
  44.7 5.1 %all-to-all-start.2 = ((f32[128,1,768]{2,1,0:T(1,128)}), f32[128,1,768]{2,1,0:T(1,128)S(1)}, u32[]{:S(2)}, u32[]{:S(2)}) async-start(f32[128,1,768]{2,1,0:T(1,128)} %bitcast.9), calls=%async_computation.2 | async-start | bytes 786432 | tf_op jit(solution)/shard_map/all_to_all | solution.py:460
  49.8 4.9 %local.8 = (f32[1152,128]{1,0:T(8,128)S(1)}, f32[8,96,128]{2,1,0:T(8,128)S(1)}, f32[1152,128]{1,0:T(8,128)}) custom-call(f32[1152,128]{1,0:T(8,128)S(1)} %get-tuple-element.58.v_ref, f32[1152,128]{1,0:T(8,128)S(1)} %bitcast.38, f32[24,576]{1,0:T(8,128)S(1)} %get-tuple-element.48.first_ref, f32[24,576]{1,0:T(8,128)S(1)} %get-tuple-element.49.second_ref, ...), custom_call_target="tpu_custom_call" | custom-call | flops 1000000000 | bytes 4000000 | tf_op jit(solution)/shard_map/local/pallas_call | solution.py:84
  54.7 6.7 %all-to-all-done.2 = f32[128,1,768]{2,1,0:T(1,128)S(1)} async-done(((f32[128,1,768]{2,1,0:T(1,128)}), f32[128,1,768]{2,1,0:T(1,128)S(1)}, u32[]{:S(2)}, u32[]{:S(2)}) %all-to-all-start.2) | async-done | bytes 393248 | tf_op jit(solution)/shard_map/all_to_all | solution.py:460
  61.4 3.1 %advance.7 = (f32[1152,128]{1,0:T(8,128)S(1)}, f32[768,128]{1,0:T(8,128)}) custom-call(f32[768,128]{1,0:T(8,128)S(1)} %bitcast.34, f32[1152,128]{1,0:T(8,128)S(1)} %get-tuple-element.59.base_ref, f32[8,96,128]{2,1,0:T(8,128)S(1)} %get-tuple-element.60.line_ref, bf16[256,1024]{1,0:T(8,128)(2,1)S(1)} %get-tuple-element.53.place_ref, ...), custom_call_target="tpu_custom_call", output_to_operand_aliasing={{0}: (1, {})} | custom-call | flops 1000000 | bytes 4000000 | tf_op jit(solution)/shard_map/advance/pallas_call | solution.py:84
  64.5 5.3 %all-to-all-start.3 = ((f32[128,1,768]{2,1,0:T(1,128)}), f32[128,1,768]{2,1,0:T(1,128)S(1)}, u32[]{:S(2)}, u32[]{:S(2)}) async-start(f32[128,1,768]{2,1,0:T(1,128)} %bitcast.11), calls=%async_computation.3 | async-start | bytes 786432 | tf_op jit(solution)/shard_map/all_to_all | solution.py:460
  69.7 6.0 %local.9 = (f32[1152,128]{1,0:T(8,128)S(1)}, f32[8,96,128]{2,1,0:T(8,128)S(1)}, f32[1152,128]{1,0:T(8,128)}) custom-call(f32[1152,128]{1,0:T(8,128)S(1)} %get-tuple-element.62.v_ref, f32[1152,128]{1,0:T(8,128)} %get-tuple-element.63.total_ref, f32[24,576]{1,0:T(8,128)S(1)} %get-tuple-element.48.first_ref, ...), custom_call_target="tpu_custom_call", output_to_operand_aliasing={{2}: (1, {})} | custom-call | flops 1000000000 | bytes 4000000 | tf_op jit(solution)/shard_map/local/pallas_call | solution.py:84
  75.7 5.5 %all-to-all-done.3 = f32[128,1,768]{2,1,0:T(1,128)S(1)} async-done(((f32[128,1,768]{2,1,0:T(1,128)}), f32[128,1,768]{2,1,0:T(1,128)S(1)}, u32[]{:S(2)}, u32[]{:S(2)}) %all-to-all-start.3) | async-done | bytes 393248 | tf_op jit(solution)/shard_map/all_to_all | solution.py:460
  81.2 3.1 %advance.8 = (f32[1152,128]{1,0:T(8,128)S(1)}, f32[768,128]{1,0:T(8,128)}) custom-call(f32[768,128]{1,0:T(8,128)S(1)} %bitcast.30, f32[1152,128]{1,0:T(8,128)S(1)} %get-tuple-element.64.base_ref, f32[8,96,128]{2,1,0:T(8,128)S(1)} %get-tuple-element.65.line_ref, bf16[256,1024]{1,0:T(8,128)(2,1)S(1)} %get-tuple-element.53.place_ref, ...), custom_call_target="tpu_custom_call", output_to_operand_aliasing={{0}: (1, {})} | custom-call | flops 1000000 | bytes 4000000 | tf_op jit(solution)/shard_map/advance/pallas_call | solution.py:84
  84.2 5.1 %all-to-all-start.4 = ((f32[128,1,768]{2,1,0:T(1,128)}), f32[128,1,768]{2,1,0:T(1,128)S(1)}, u32[]{:S(2)}, u32[]{:S(2)}) async-start(f32[128,1,768]{2,1,0:T(1,128)} %bitcast.13), calls=%async_computation.4 | async-start | bytes 786432 | tf_op jit(solution)/shard_map/all_to_all | solution.py:460
  89.3 6.0 %local.10 = (f32[1152,128]{1,0:T(8,128)S(1)}, f32[8,96,128]{2,1,0:T(8,128)S(1)}, f32[1152,128]{1,0:T(8,128)}) custom-call(f32[1152,128]{1,0:T(8,128)S(1)} %get-tuple-element.67.v_ref, f32[1152,128]{1,0:T(8,128)} %get-tuple-element.68.total_ref, f32[24,576]{1,0:T(8,128)S(1)} %get-tuple-element.48.first_ref, ...), custom_call_target="tpu_custom_call", output_to_operand_aliasing={{2}: (1, {})} | custom-call | flops 1000000000 | bytes 4000000 | tf_op jit(solution)/shard_map/local/pallas_call | solution.py:84
  95.3 5.6 %all-to-all-done.4 = f32[128,1,768]{2,1,0:T(1,128)S(1)} async-done(((f32[128,1,768]{2,1,0:T(1,128)}), f32[128,1,768]{2,1,0:T(1,128)S(1)}, u32[]{:S(2)}, u32[]{:S(2)}) %all-to-all-start.4) | async-done | bytes 393248 | tf_op jit(solution)/shard_map/all_to_all | solution.py:460
  100.9 3.1 %advance.9 = (f32[1152,128]{1,0:T(8,128)S(1)}, f32[768,128]{1,0:T(8,128)}) custom-call(f32[768,128]{1,0:T(8,128)S(1)} %bitcast.31, f32[1152,128]{1,0:T(8,128)S(1)} %get-tuple-element.69.base_ref, f32[8,96,128]{2,1,0:T(8,128)S(1)} %get-tuple-element.70.line_ref, bf16[256,1024]{1,0:T(8,128)(2,1)S(1)} %get-tuple-element.53.place_ref, ...), custom_call_target="tpu_custom_call", output_to_operand_aliasing={{0}: (1, {})} | custom-call | flops 1000000 | bytes 4000000 | tf_op jit(solution)/shard_map/advance/pallas_call | solution.py:84
  104.0 5.1 %all-to-all-start.5 = ((f32[128,1,768]{2,1,0:T(1,128)}), f32[128,1,768]{2,1,0:T(1,128)S(1)}, u32[]{:S(2)}, u32[]{:S(2)}) async-start(f32[128,1,768]{2,1,0:T(1,128)} %bitcast.15), calls=%async_computation.5 | async-start | bytes 786432 | tf_op jit(solution)/shard_map/all_to_all | solution.py:460
  109.1 6.0 %local.11 = (f32[1152,128]{1,0:T(8,128)S(1)}, f32[8,96,128]{2,1,0:T(8,128)S(1)}, f32[1152,128]{1,0:T(8,128)}) custom-call(f32[1152,128]{1,0:T(8,128)S(1)} %get-tuple-element.72.v_ref, f32[1152,128]{1,0:T(8,128)} %get-tuple-element.73.total_ref, f32[24,576]{1,0:T(8,128)S(1)} %get-tuple-element.48.first_ref, ...), custom_call_target="tpu_custom_call", output_to_operand_aliasing={{2}: (1, {})} | custom-call | flops 1000000000 | bytes 4000000 | tf_op jit(solution)/shard_map/local/pallas_call | solution.py:84
  115.1 5.6 %all-to-all-done.5 = f32[128,1,768]{2,1,0:T(1,128)S(1)} async-done(((f32[128,1,768]{2,1,0:T(1,128)}), f32[128,1,768]{2,1,0:T(1,128)S(1)}, u32[]{:S(2)}, u32[]{:S(2)}) %all-to-all-start.5) | async-done | bytes 393248 | tf_op jit(solution)/shard_map/all_to_all | solution.py:460
  120.7 3.1 %advance.10 = (f32[1152,128]{1,0:T(8,128)S(1)}, f32[768,128]{1,0:T(8,128)}) custom-call(f32[768,128]{1,0:T(8,128)S(1)} %bitcast.32, f32[1152,128]{1,0:T(8,128)S(1)} %get-tuple-element.74.base_ref, f32[8,96,128]{2,1,0:T(8,128)S(1)} %get-tuple-element.75.line_ref, bf16[256,1024]{1,0:T(8,128)(2,1)S(1)} %get-tuple-element.53.place_ref, ...), custom_call_target="tpu_custom_call", output_to_operand_aliasing={{0}: (1, {})} | custom-call | flops 1000000 | bytes 4000000 | tf_op jit(solution)/shard_map/advance/pallas_call | solution.py:84
  123.8 5.3 %all-to-all-start.6 = ((f32[128,1,768]{2,1,0:T(1,128)}), f32[128,1,768]{2,1,0:T(1,128)S(1)}, u32[]{:S(2)}, u32[]{:S(2)}) async-start(f32[128,1,768]{2,1,0:T(1,128)} %bitcast.17), calls=%async_computation.6 | async-start | bytes 786432 | tf_op jit(solution)/shard_map/all_to_all | solution.py:460
  129.1 6.0 %local.12 = (f32[1152,128]{1,0:T(8,128)S(1)}, f32[8,96,128]{2,1,0:T(8,128)S(1)}, f32[1152,128]{1,0:T(8,128)}) custom-call(f32[1152,128]{1,0:T(8,128)S(1)} %get-tuple-element.77.v_ref.refs_1_, f32[1152,128]{1,0:T(8,128)} %get-tuple-element.78.total_ref, f32[24,576]{1,0:T(8,128)S(1)} %get-tuple-element.48.first_ref, ...), custom_call_target="tpu_custom_call", output_to_operand_aliasing={{2}: (1, {})} | custom-call | flops 1000000000 | bytes 4000000 | tf_op jit(solution)/shard_map/local/pallas_call | solution.py:84
  135.1 5.4 %all-to-all-done.6 = f32[128,1,768]{2,1,0:T(1,128)S(1)} async-done(((f32[128,1,768]{2,1,0:T(1,128)}), f32[128,1,768]{2,1,0:T(1,128)S(1)}, u32[]{:S(2)}, u32[]{:S(2)}) %all-to-all-start.6) | async-done | bytes 393248 | tf_op jit(solution)/shard_map/all_to_all | solution.py:460
  140.5 3.1 %advance.11 = (f32[1152,128]{1,0:T(8,128)S(1)}, f32[768,128]{1,0:T(8,128)}) custom-call(f32[768,128]{1,0:T(8,128)S(1)} %bitcast.29, f32[1152,128]{1,0:T(8,128)S(1)} %get-tuple-element.79.base_ref, f32[8,96,128]{2,1,0:T(8,128)S(1)} %get-tuple-element.80.line_ref, bf16[256,1024]{1,0:T(8,128)(2,1)S(1)} %get-tuple-element.53.place_ref, ...), custom_call_target="tpu_custom_call", output_to_operand_aliasing={{0}: (1, {})} | custom-call | flops 1000000 | bytes 4000000 | tf_op jit(solution)/shard_map/advance/pallas_call | solution.py:84
  143.6 5.1 %all-to-all-start.7 = ((f32[128,1,768]{2,1,0:T(1,128)}), f32[128,1,768]{2,1,0:T(1,128)S(1)}, u32[]{:S(2)}, u32[]{:S(2)}) async-start(f32[128,1,768]{2,1,0:T(1,128)} %bitcast.21), calls=%async_computation.7 | async-start | bytes 786432 | tf_op jit(solution)/shard_map/all_to_all | solution.py:460
  149.7 6.6 %local.13 = (f32[1152,128]{1,0:T(8,128)S(1)}, f32[1152,128]{1,0:T(8,128)}, f32[1152,128]{1,0:T(8,128)S(1)}) custom-call(f32[1152,128]{1,0:T(8,128)S(1)} %get-tuple-element.81.v_ref, f32[1152,128]{1,0:T(8,128)} %get-tuple-element.82.total_ref, f32[24,576]{1,0:T(8,128)S(1)} %get-tuple-element.48.first_ref, ...), custom_call_target="tpu_custom_call", output_to_operand_aliasing={{1}: (1, {})} | custom-call | flops 1000000000 | bytes 4000000 | tf_op jit(solution)/shard_map/local/pallas_call | solution.py:84
  156.4 3.9 %all-to-all-done.7 = f32[128,1,768]{2,1,0:T(1,128)S(1)} async-done(((f32[128,1,768]{2,1,0:T(1,128)}), f32[128,1,768]{2,1,0:T(1,128)S(1)}, u32[]{:S(2)}, u32[]{:S(2)}) %all-to-all-start.7) | async-done | bytes 393248 | tf_op jit(solution)/shard_map/all_to_all | solution.py:460
  160.3 1.7 finish.1
  162.0 14.9 %all_to_all.45 = f32[128,1,128]{2,1,0:T(1,128)S(1)} all-to-all(f32[128,1,128]{2,1,0:T(1,128)S(1)} %bitcast.41), channel_id=1, replica_groups=mesh['grp'=2,'dev'=64] {'grp','dev'}, dimensions={0} | all-to-all | bytes 131072 | tf_op jit(solution)/shard_map/all_to_all | solution.py:460
  (33 shorter events, 6.2 us)
Async XLA Ops:
  0.6 0.7 copy-start.3
  1.3 0.7 copy-start.7
  3.2 11.9 %copy-start.5 = (f32[4,8,128]{2,1,0:T(8,128)S(1)}, f32[4,8,128]{2,1,0:T(8,128)}, u32[]{:S(2)}) copy-start(f32[4,8,128]{2,1,0:T(8,128)} %param.15) | copy-start | bytes 49156
  3.2 11.9 %copy-start.6 = (f32[24,24]{1,0:T(8,128)S(1)}, f32[24,24]{1,0:T(8,128)}, u32[]{:S(2)}) copy-start(f32[24,24]{1,0:T(8,128)} %ham_ref.1) | copy-start | bytes 6916
  3.3 20.3 %all-to-all-start = ((f32[128,1,128]{2,1,0:T(1,128)}), f32[128,1,128]{2,1,0:T(1,128)S(1)}, u32[]{:S(2)}, u32[]{:S(2)}) async-start(f32[128,1,128]{2,1,0:T(1,128)} %bitcast.5), calls=%async_computation | async-start | bytes 131072 | tf_op jit(solution)/shard_map/all_to_all | solution.py:460
  15.1 0.7 copy-start.9
  15.1 0.7 copy-start.10
  15.1 0.7 copy-start.11
  15.8 7.7 %copy-start = (f32[2,24,24,128]{3,2,1,0:T(8,128)S(1)}, f32[2,24,24,128]{3,2,1,0:T(8,128)}, u32[]{:S(2)}) copy-start(f32[2,24,24,128]{3,2,1,0:T(8,128)} %param.9) | copy-start | bytes 1769476
  16.3 92.8 %copy-start.12 = (f32[24,576]{1,0:T(8,128)}, f32[24,576]{1,0:T(8,128)S(1)}, u32[]{:S(2)}) copy-start(f32[24,576]{1,0:T(8,128)S(1)} %get-tuple-element.49.second_ref) | copy-start | bytes 165892
  25.1 4.9 %copy-start.8 = (s32[8,128]{1,0:T(8,128)S(1)}, s32[8,128]{1,0:T(8,128)}, u32[]{:S(2)}) copy-start(s32[8,128]{1,0:T(8,128)} %src_ref.15) | copy-start | bytes 12292
  25.1 16.5 %all-to-all-start.1 = ((f32[128,1,768]{2,1,0:T(1,128)}), f32[128,1,768]{2,1,0:T(1,128)S(1)}, u32[]{:S(2)}, u32[]{:S(2)}) async-start(f32[128,1,768]{2,1,0:T(1,128)} %bitcast.7), calls=%async_computation.1 | async-start | bytes 786432 | tf_op jit(solution)/shard_map/all_to_all | solution.py:460
  30.0 0.7 copy-start.4
  44.7 16.7 %all-to-all-start.2 = ((f32[128,1,768]{2,1,0:T(1,128)}), f32[128,1,768]{2,1,0:T(1,128)S(1)}, u32[]{:S(2)}, u32[]{:S(2)}) async-start(f32[128,1,768]{2,1,0:T(1,128)} %bitcast.9), calls=%async_computation.2 | async-start | bytes 786432 | tf_op jit(solution)/shard_map/all_to_all | solution.py:460
  64.5 16.7 %all-to-all-start.3 = ((f32[128,1,768]{2,1,0:T(1,128)}), f32[128,1,768]{2,1,0:T(1,128)S(1)}, u32[]{:S(2)}, u32[]{:S(2)}) async-start(f32[128,1,768]{2,1,0:T(1,128)} %bitcast.11), calls=%async_computation.3 | async-start | bytes 786432 | tf_op jit(solution)/shard_map/all_to_all | solution.py:460
  84.2 16.7 %all-to-all-start.4 = ((f32[128,1,768]{2,1,0:T(1,128)}), f32[128,1,768]{2,1,0:T(1,128)S(1)}, u32[]{:S(2)}, u32[]{:S(2)}) async-start(f32[128,1,768]{2,1,0:T(1,128)} %bitcast.13), calls=%async_computation.4 | async-start | bytes 786432 | tf_op jit(solution)/shard_map/all_to_all | solution.py:460
  104.0 16.7 %all-to-all-start.5 = ((f32[128,1,768]{2,1,0:T(1,128)}), f32[128,1,768]{2,1,0:T(1,128)S(1)}, u32[]{:S(2)}, u32[]{:S(2)}) async-start(f32[128,1,768]{2,1,0:T(1,128)} %bitcast.15), calls=%async_computation.5 | async-start | bytes 786432 | tf_op jit(solution)/shard_map/all_to_all | solution.py:460
  123.8 11.3 %copy-start.1 = (f32[1152,128]{1,0:T(8,128)}, f32[1152,128]{1,0:T(8,128)S(1)}, u32[]{:S(2)}) copy-start(f32[1152,128]{1,0:T(8,128)S(1)} %get-tuple-element.77.v_ref.refs_1_) | copy-start | bytes 1769476
  123.8 5.3 %copy-start.13 = (f32[24,576]{1,0:T(8,128)S(1)}, f32[24,576]{1,0:T(8,128)}, u32[]{:S(2)}) copy-start(f32[24,576]{1,0:T(8,128)} %copy-done.12) | copy-start | bytes 165892
  123.8 16.7 %all-to-all-start.6 = ((f32[128,1,768]{2,1,0:T(1,128)}), f32[128,1,768]{2,1,0:T(1,128)S(1)}, u32[]{:S(2)}, u32[]{:S(2)}) async-start(f32[128,1,768]{2,1,0:T(1,128)} %bitcast.17), calls=%async_computation.6 | async-start | bytes 786432 | tf_op jit(solution)/shard_map/all_to_all | solution.py:460
  143.6 5.1 %copy-start.14 = (f32[24,576]{1,0:T(8,128)S(1)}, f32[24,576]{1,0:T(8,128)}, u32[]{:S(2)}) copy-start(f32[24,576]{1,0:T(8,128)} %copy-done.12) | copy-start | bytes 165892
  143.6 16.7 %all-to-all-start.7 = ((f32[128,1,768]{2,1,0:T(1,128)}), f32[128,1,768]{2,1,0:T(1,128)S(1)}, u32[]{:S(2)}, u32[]{:S(2)}) async-start(f32[128,1,768]{2,1,0:T(1,128)} %bitcast.21), calls=%async_computation.7 | async-start | bytes 786432 | tf_op jit(solution)/shard_map/all_to_all | solution.py:460
  148.7 1.1 copy-start.2
